TPU v7x, 32 devices: a whole 2x2x4 slice. The times are simulated.
32 devices in a mesh: grp: 1, tok: 32 (over z, y, x, core).
Axes of the slice: x: 2, y: 2, z: 4, core: 2. Of those that a mesh axis runs over, the one named last changes fastest.
Arguments:
- queries: bfloat16 [4096, 2048], P(('grp', 'tok')), may hold values from -16 to 16
- keys: bfloat16 [4096, 2048], P(('grp', 'tok')), may hold values from -16 to 16
- values: bfloat16 [4096, 2048], P(('grp', 'tok')), may hold values from -6 to 6
- segment: int32 [4096], P(('grp', 'tok')), may hold values from 0 to 41, never falling along the last dimension, each value on 1 to 256 neighbouring positions
- rates: float32 [4096, 2], P(('grp', 'tok')), may hold values from 0.00046875 to 0.0046875
- fast_one: bfloat16 [2048, 512], P(('grp', 'tok')), may hold values from -0.1875 to 0.1875
- fast_three: bfloat16 [2048, 512], P(('grp', 'tok')), may hold values from -0.1875 to 0.1875
- fast_two: bfloat16 [2048, 512], P(('grp', 'tok')), may hold values from -0.25 to 0.25
Outputs:
- attended: bfloat16 [4096, 2048], P(('grp', 'tok'))
- fast_out: bfloat16 [4096, 2048], P(('grp', 'tok'))
Inputs may be any that keep to these rules, and one draw needn't show every extreme that they name: `segment`: exemplar numbers never fall along the tokens; each exemplar covers 1 to 256 consecutive tokens.
All inputs are finite; a program needn't handle non-finite values.
Results may differ from a plain program's by a relative error of at most 0.0084.
Values may be sent and summed in bfloat16 or wider, within the bound.
A program may use at most 128 MiB of HBM per device.

v0:
```python
import functools
import math

import jax
import jax.numpy as jnp
from jax import lax
from jax.experimental import pallas as pl
from jax.experimental.pallas import tpu as pltpu
from jax.sharding import PartitionSpec as P

D = 2048
ATT_HEADS = 16
FAST_HEADS = 2
FAST_DIM = 1024
FAST_HID = 512
WINDOW = 128


EPS = 1e-06


def axis_orders(count):
    bits = count.bit_length() - 1
    rest = list(range(1, bits))
    return [[0] + rest[m:] + rest[:m] if rest else [0] for m in range(3)]


def bit_of(index, bit):
    return lax.rem(lax.div(index, jnp.int32(1 << bit)), jnp.int32(2))


def coordinate(index, bit, bits):
    here = bit_of(index, bit)
    if bits >= 3 and bit == bits - 2:
        top = bit_of(index, bits - 1)
        here = here + top - 2 * here * top
    return here


def partner_of(me, bit, bits):
    other = me + (1 - 2 * bit_of(me, bit)) * (1 << bit)
    if bits >= 3 and bit == bits - 1:
        other = other + (1 - 2 * bit_of(me, bit - 1)) * (1 << (bit - 1))
    return other


def block_of(index, order):
    total = jnp.int32(0)
    for bit in order:
        total = total * 2 + coordinate(index, bit, len(order))
    return total


def device_of(block, order):
    bits = len(order)
    index = 0
    for place, bit in enumerate(reversed(order)):
        index += ((block >> place) & 1) << bit
    if bits >= 3 and (index >> (bits - 1)) & 1:
        index ^= 1 << (bits - 2)
    return index


def greet(me, bits, others=()):
    barrier = pltpu.get_barrier_semaphore()
    partners = [partner_of(me, bit, bits) for bit in range(bits)] + list(others)
    for partner in partners:
        pl.semaphore_signal(
            barrier,
            inc=1,
            device_id={"tok": partner},
            device_id_type=pl.DeviceIdType.MESH,
        )
    pl.semaphore_wait(barrier, len(partners))


def remote(src, dst, send_sem, recv_sem, partner):
    return pltpu.make_async_remote_copy(
        src_ref=src,
        dst_ref=dst,
        send_sem=send_sem,
        recv_sem=recv_sem,
        device_id={"tok": partner},
        device_id_type=pl.DeviceIdType.MESH,
    )


def gather_kernel(count, *refs):
    orders = axis_orders(count)
    bits = count.bit_length() - 1
    parts = refs[:3]
    q_ref, k_ref, v_ref, seg_col, seg_row = refs[3:8]
    outs, att_ref = refs[8:11], refs[11]
    held, old_k, old_v, old_seg, local_sem, send_sem, recv_sem, halo_send, halo_recv = refs[12:]
    me = lax.axis_index("tok")
    after, before = lax.rem(me + 1, count), lax.rem(me + count - 1, count)
    own = [block_of(me, orders[m]) for m in range(3)]
    local = [
        pltpu.make_async_copy(parts[m], held.at[m, own[m]], local_sem.at[m]) for m in range(3)
    ]
    for copy in local:
        copy.start()
    greet(me, bits, (after, before))
    copies = {}

    def send(m, step):
        bit = orders[m][bits - 1 - step]
        size = 1 << step
        start = lax.div(own[m], jnp.int32(size)) * size
        here = held.at[m, pl.ds(start, size)]
        copies[m, step] = remote(
            here, here, send_sem.at[m, step], recv_sem.at[m, step], partner_of(me, bit, bits)
        )
        copies[m, step].start()

    for m in range(3):
        local[m].wait()
        send(m, 0)
    halo = [
        remote(src, dst, halo_send.at[i], halo_recv.at[i], after)
        for i, (src, dst) in enumerate(((seg_row, old_seg), (k_ref, old_k), (v_ref, old_v)))
    ]
    for copy in halo:
        copy.start()

    rows = q_ref.shape[0]
    dim = D // ATT_HEADS
    scale = 1.0 / math.sqrt(dim)

    def attend_heads(first, last):
        row = lax.broadcasted_iota(jnp.int32, (rows, rows), 0)
        col = lax.broadcasted_iota(jnp.int32, (rows, rows), 1)
        own_seg = seg_col[...]
        now_ok = (col <= row) & (row - col < WINDOW) & (own_seg == seg_row[0:1, :])
        old_ok = (row - col + rows < WINDOW) & (own_seg == old_seg[0:1, :]) & (row + me * rows >= row + rows)

        def one(head, carry):
            lanes = pl.ds(pl.multiple_of(head * dim, dim), dim)
            q = q_ref[:, lanes]

            def score(keys, allowed):
                dots = lax.dot_general(
                    q, keys, (((1,), (1,)), ((), ())), preferred_element_type=jnp.float32
                )
                return jnp.where(allowed, dots * scale, jnp.float32(-1e30))

            old, now = score(old_k[:, lanes], old_ok), score(k_ref[:, lanes], now_ok)
            top = jnp.maximum(
                jnp.max(old, axis=1, keepdims=True), jnp.max(now, axis=1, keepdims=True)
            )
            old = jnp.where(old_ok, jnp.exp(old - top), jnp.float32(0.0))
            now = jnp.where(now_ok, jnp.exp(now - top), jnp.float32(0.0))
            total = jnp.sum(old, axis=1, keepdims=True) + jnp.sum(now, axis=1, keepdims=True)
            out = jnp.dot(
                (old / total).astype(jnp.bfloat16),
                old_v[:, lanes],
                preferred_element_type=jnp.float32,
            ) + jnp.dot(
                (now / total).astype(jnp.bfloat16),
                v_ref[:, lanes],
                preferred_element_type=jnp.float32,
            )
            att_ref[:, lanes] = out.astype(jnp.bfloat16)
            return carry

        lax.fori_loop(first, last, one, 0)

    for step in range(bits):
        if step == bits - 2:
            for copy in halo:
                copy.wait_recv()
            attend_heads(0, 12)
        if step == bits - 1:
            attend_heads(12, ATT_HEADS)
        for m in range(3):
            copies[m, step].wait_recv()
            if step + 1 < bits:
                send(m, step + 1)
            else:
                for block in range(count):
                    outs[m][device_of(block, orders[m])] = held[m, block]
    for copy in list(copies.values()) + halo:
        copy.wait_send()


def gather_weights(weights, queries, keys, values, segment, count):
    rows, cols = weights[0].shape
    tokens = queries.shape[0]
    bits = count.bit_length() - 1
    seg_row = jnp.broadcast_to(segment[None, :], (8, tokens))
    outs = pl.pallas_call(
        functools.partial(gather_kernel, count),
        out_shape=[jax.ShapeDtypeStruct((count, rows, cols), jnp.bfloat16)] * 3
        + [jax.ShapeDtypeStruct(queries.shape, jnp.bfloat16)],
        in_specs=[pl.BlockSpec(memory_space=pltpu.VMEM)] * 8,
        out_specs=[pl.BlockSpec(memory_space=pltpu.VMEM)] * 4,
        scratch_shapes=[
            pltpu.VMEM((3, count, rows, cols), jnp.bfloat16),
            pltpu.VMEM(keys.shape, jnp.bfloat16),
            pltpu.VMEM(values.shape, jnp.bfloat16),
            pltpu.VMEM((8, tokens), jnp.int32),
            pltpu.SemaphoreType.DMA((3,)),
            pltpu.SemaphoreType.DMA((3, bits)),
            pltpu.SemaphoreType.DMA((3, bits)),
            pltpu.SemaphoreType.DMA((3,)),
            pltpu.SemaphoreType.DMA((3,)),
        ],
        compiler_params=pltpu.CompilerParams(collective_id=0, has_side_effects=True),
        cost_estimate=pl.CostEstimate(flops=0, bytes_accessed=100_000_000, transcendentals=0),
    )(*weights, queries, keys, values, segment[:, None], seg_row)
    return [out.reshape(count * rows, cols) for out in outs[:3]], outs[3]


def update_kernel(count, *refs):
    orders = axis_orders(count)
    bits = count.bit_length() - 1
    hiddens, tokens = refs[:3], (refs[3], refs[3], refs[4])
    olds, outs = refs[5:8], refs[8:11]
    total, staged, landed, send_sem, recv_sem = refs[11:]
    rows, cols = olds[0].shape
    me = lax.axis_index("tok")
    own = [block_of(me, orders[m]) for m in range(3)]
    copies = {}

    def first_kept(m, step):
        size = count >> (step + 1)
        return lax.div(own[m], jnp.int32(size)) * size

    def half_start(m):
        return lax.div(own[m], jnp.int32(count // 2)) * (count // 2)

    def gradient(m, block, store):
        lead = count // 2 * rows
        chunk = 128
        each = chunk // rows
        lanes = pl.ds(pl.multiple_of(lax.div(block * rows, FAST_HID) * cols, cols), cols)
        wide = tokens[m][:, lanes]

        def one(i, carry):
            at = pl.ds(pl.multiple_of(block * rows + i * chunk, chunk), chunk)
            part = jnp.dot(hiddens[m][at, :], wide, preferred_element_type=jnp.float32)
            store(i * each, each, part.reshape(each, rows, cols))
            return carry

        lax.fori_loop(0, lead // chunk, one, 0)

    def stage_first(m, at, size, part):
        staged[m, pl.ds(at, size)] = part.astype(jnp.bfloat16)

    def keep_first(m, at, size, part):
        total[m, pl.ds(at, size)] = part

    def send_half(m, step):
        bit = orders[m][step]
        size = count >> (step + 1)
        place = pl.ds(count - 2 * size, size)
        copies[m, step] = remote(
            staged.at[m, place],
            landed.at[m, place],
            send_sem.at[m, step],
            recv_sem.at[m, step],
            partner_of(me, bit, bits),
        )
        copies[m, step].start()

    def pass_on(m, step):
        size = count >> (step + 1)
        base, keep = first_kept(m, step - 1), first_kept(m, step)
        away = 2 * base + size - keep
        half = half_start(m)
        below = count - 4 * size

        def sum_of(block):
            other = landed[m, below + block - base].astype(jnp.float32)
            return total[m, block - half] + other

        def stage(i, carry):
            staged[m, count - 2 * size + i] = sum_of(away + i).astype(jnp.bfloat16)
            return carry

        def hold(i, carry):
            total[m, keep - half + i] = sum_of(keep + i)
            return carry

        lax.fori_loop(0, size, stage, 0)
        send_half(m, step)
        lax.fori_loop(0, size, hold, 0)

    def send_new(m, step):
        bit = orders[m][bits - 1 - step]
        size = 1 << step
        start = lax.div(own[m], jnp.int32(size)) * size
        here = outs[m].at[pl.ds(start, size)]
        at = bits + step
        copies[m, at] = remote(
            here, here, send_sem.at[m, at], recv_sem.at[m, at], partner_of(me, bit, bits)
        )
        copies[m, at].start()

    for m in range(3):
        gradient(m, count // 2 - half_start(m), functools.partial(stage_first, m))
        if m == 0:
            greet(me, bits)
        send_half(m, 0)
    for m in range(3):
        gradient(m, half_start(m), functools.partial(keep_first, m))
    for step in range(1, bits):
        for m in range(3):
            copies[m, step - 1].wait_recv()
            pass_on(m, step)
    for m in range(3):
        copies[m, bits - 1].wait_recv()
        grad = total[m, own[m] - half_start(m)] + landed[m, count - 2].astype(jnp.float32)
        old = olds[m][...].astype(jnp.float32)
        update = old - grad
        old_len = jnp.sqrt(jnp.sum(old * old, axis=1, keepdims=True))
        new_len = jnp.sqrt(jnp.sum(update * update, axis=1, keepdims=True) + EPS)
        outs[m][own[m]] = (update * (old_len / new_len)).astype(jnp.bfloat16)
        send_new(m, 0)
    for step in range(bits):
        for m in range(3):
            copies[m, bits + step].wait_recv()
            if step + 1 < bits:
                send_new(m, step + 1)
    for copy in copies.values():
        copy.wait_send()


def update_weights(hiddens, keys, values, olds, count):
    rows, cols = olds[0].shape
    bits = count.bit_length() - 1
    shape = (count, rows, cols)
    return pl.pallas_call(
        functools.partial(update_kernel, count),
        out_shape=[jax.ShapeDtypeStruct(shape, jnp.bfloat16)] * 3,
        in_specs=[pl.BlockSpec(memory_space=pltpu.VMEM)] * 8,
        out_specs=[pl.BlockSpec(memory_space=pltpu.VMEM)] * 3,
        scratch_shapes=[
            pltpu.VMEM((3, count // 2, rows, cols), jnp.float32),
            pltpu.VMEM((3, count, rows, cols), jnp.bfloat16),
            pltpu.VMEM((3, count, rows, cols), jnp.bfloat16),
            pltpu.SemaphoreType.DMA((3, 2 * bits)),
            pltpu.SemaphoreType.DMA((3, 2 * bits)),
        ],
        compiler_params=pltpu.CompilerParams(collective_id=1, has_side_effects=True),
        cost_estimate=pl.CostEstimate(flops=0, bytes_accessed=200_000_000, transcendentals=0),
    )(*hiddens, keys, values, *olds)


def project(rows, weight):
    matrix = weight.reshape(FAST_HEADS, FAST_DIM, weight.shape[1])
    return jnp.einsum("thd,hdc->thc", rows, matrix, preferred_element_type=jnp.float32)


def hidden_first(hidden):
    return hidden.astype(jnp.bfloat16).reshape(hidden.shape[0], FAST_HEADS * FAST_HID).T


def per_device(queries, keys, values, segment, rates, fast_one, fast_three, fast_two):
    count = queries.shape[0]
    devices = lax.axis_size("tok")
    shard = lax.axis_index("tok")
    width = FAST_HEADS * FAST_DIM
    key_fast = keys.reshape(count, FAST_HEADS, FAST_DIM)
    value_fast = values.reshape(count, FAST_HEADS, FAST_DIM)
    query_fast = queries.reshape(count, FAST_HEADS, FAST_DIM)
    fulls, attended = gather_weights(
        (fast_one, fast_three, fast_two), queries, keys, values, segment, devices
    )
    full_one, full_three, full_two = fulls
    rate = rates[:, :, None]
    a_one = project(key_fast, full_one)
    a_three = project(key_fast, full_three)
    sig = jax.nn.sigmoid(a_one)
    weighted = (-rate * a_one * sig * a_three).astype(jnp.bfloat16)
    back = -rate * project(value_fast, full_two)
    delta_one = (back * a_three * sig * (1.0 + a_one * (1.0 - sig))).astype(jnp.bfloat16)
    delta_three = (back * a_one * sig).astype(jnp.bfloat16)
    hiddens = [hidden_first(hidden) for hidden in (delta_one, delta_three, weighted)]
    rows_here = FAST_HEADS * FAST_HID // devices
    olds = []
    for m, order in enumerate(axis_orders(devices)):
        start = block_of(shard, order) * rows_here
        own_cols = lax.dynamic_slice(
            fulls[m].reshape(FAST_HEADS, FAST_DIM, FAST_HID),
            (start // FAST_HID, jnp.int32(0), start % FAST_HID),
            (1, FAST_DIM, rows_here),
        )
        olds.append(own_cols[0].T)
    news = update_weights(hiddens, keys, values, olds, devices)
    new_one, new_three, new_two = [n.reshape(FAST_HEADS, FAST_HID, FAST_DIM) for n in news]
    b_one = jnp.einsum("thd,hcd->thc", query_fast, new_one, preferred_element_type=jnp.float32)
    b_three = jnp.einsum("thd,hcd->thc", query_fast, new_three, preferred_element_type=jnp.float32)
    mixed = (jax.nn.silu(b_one) * b_three).astype(jnp.bfloat16)
    fast_out = jnp.einsum("thc,hcd->thd", mixed, new_two, preferred_element_type=jnp.float32)
    fast_out = fast_out.reshape(count, width).astype(jnp.bfloat16)
    return (attended, fast_out)


def solution(mesh):
    placed = (
        P(("grp", "tok"), None),
        P(("grp", "tok"), None),
        P(("grp", "tok"), None),
        P(("grp", "tok")),
        P(("grp", "tok"), None),
        P(("grp", "tok"), None),
        P(("grp", "tok"), None),
        P(("grp", "tok"), None),
    )
    return jax.shard_map(
        per_device,
        mesh=mesh,
        in_specs=placed,
        out_specs=(P(("grp", "tok"), None), P(("grp", "tok"), None)),
        check_vma=False,
    )
```

profile of v0, /device:TPU:1, one launch (start us, length us, event | category | flops | bytes accessed | tf_op | source)
XLA Modules:
  0.0 166.9 jit_solution(3684442086085092469)
XLA Ops:
  0.7 1.4 copy.10.refs_6_
  2.1 1.2 broadcast_in_dim.5.refs_7_
  3.4 0.0 copy-start.6
  3.4 0.0 copy-start.1
  3.4 56.0 %shard_map.95 = (bf16[32,64,512]{2,1,0:T(8,128)(2,1)}, bf16[32,64,512]{2,1,0:T(8,128)(2,1)}, bf16[32,64,512]{2,1,0:T(8,128)(2,1)}, bf16[128,2048]{1,0:T(8,128)(2,1)}) custom-call(bf16[64,512]{1,0:T(8,128)(2,1)} %refs_0_.1, bf16[64,512]{1,0:T(8,128)(2,1)} %refs_1_.1, bf16[64,512]{1,0:T(8,128)(2,1)} %refs_2_.1, bf16[128,2048]{1,0:T(8,128)(2,1)} %refs_3_.2, ...), custom_call_target="tpu_custom_call" | custom-call | bytes 100000000 | tf_op jit(solution)/shard_map/pallas_call | solution.py:191
  59.4 1.1 constant_dynamic-slice_fusion
  60.5 0.7 copy.32
  61.2 1.1 constant_dynamic-slice_fusion.1
  62.3 0.7 copy.31
  63.1 0.0 copy-start
  63.1 0.0 copy-start.2
  63.1 1.2 constant_dynamic-slice_fusion.2
  64.3 0.7 copy.30
  65.0 0.0 copy-done.6
  65.0 0.0 copy-done.1
  65.0 2.5 %fusion = f32[128,2,512]{0,2,1:T(8,128)S(1)} fusion(bf16[2,1024,512]{2,1,0:T(8,128)(2,1)} %bitcast.73, bf16[16,2,8,1024]{3,2,1,0:T(8,128)(2,1)S(1)} %bitcast.69, f32[128,2]{0,1:T(2,128)S(1)} %neg.12), kind=kOutput, calls=%fused_computation.6 | convolution fusion | flops 268566528 | bytes 3146752 | tf_op jit(solution)/shard_map/thd,hdc->thc/dot_general | solution.py:352
  67.6 0.0 copy-start.5
  67.6 0.0 copy-done
  67.6 0.0 copy-done.2
  67.6 0.9 convolution_bitcast_fusion.2
  68.5 0.6 copy-done.5
  69.2 1.9 %multiply_convert_fusion = (bf16[128,2,512]{0,2,1:T(8,128)(2,1)}, bf16[128,2,512]{0,2,1:T(8,128)(2,1)}, bf16[128,2,512]{0,2,1:T(8,128)(2,1)}) fusion(f32[128,2,512]{0,2,1:T(8,128)S(1)} %convolution_bitcast_fusion.2, f32[128,2]{0,1:T(2,128)S(1)} %neg.12, f32[128,2,512]{0,2,1:T(8,128)S(1)} %fusion, bf16[2,1024,512]{2,1,0:T(8,128)(2,1)S(1)} %bitcast.85, ...), kind=kOutput, calls=%fused_computation.18 | convolution fusion | flops 270663680 | bytes 4457472 | tf_op jit(solution)/shard_map/thd,hdc->thc/dot_general | solution.py:352
  71.0 0.0 copy-start.3
  71.0 87.8 %shard_map.96 = (bf16[32,32,1024]{2,1,0:T(8,128)(2,1)}, bf16[32,32,1024]{2,1,0:T(8,128)(2,1)}, bf16[32,32,1024]{2,1,0:T(8,128)(2,1)}) custom-call(bf16[1024,128]{1,0:T(8,128)(2,1)} %bitcast.82, bf16[1024,128]{1,0:T(8,128)(2,1)} %bitcast.83, bf16[1024,128]{1,0:T(8,128)(2,1)} %bitcast.81, bf16[128,2048]{1,0:T(8,128)(2,1)} %refs_3_.3, ...), custom_call_target="tpu_custom_call" | custom-call | bytes 200000000 | tf_op jit(solution)/shard_map/pallas_call | solution.py:333
  158.9 0.0 copy-done.3
  158.9 0.3 copy.33
  159.2 2.3 %convolution_bitcast_fusion.1 = f32[128,2,512]{0,2,1:T(8,128)S(1)} fusion(bf16[2,512,1024]{2,1,0:T(8,128)(2,1)} %bitcast.74, bf16[128,2,1024]{0,2,1:T(8,128)(2,1)S(1)} %bitcast.75), kind=kOutput, calls=%fused_computation.2 | convolution fusion | flops 268435456 | bytes 3145728 | tf_op jit(solution)/shard_map/thd,hcd->thc/dot_general | solution.py:392
  161.5 0.0 copy-start.4
  161.5 3.6 %convolution_convert_fusion = bf16[2,1024,128]{2,1,0:T(8,128)(2,1)S(1)} fusion(bf16[2,512,1024]{2,1,0:T(8,128)(2,1)} %bitcast.88, bf16[2,512,1024]{2,1,0:T(8,128)(2,1)} %bitcast.87, bf16[128,2,1024]{0,2,1:T(8,128)(2,1)S(1)} %bitcast.76, f32[128,2,512]{0,2,1:T(8,128)S(1)} %convolution_bitcast_fusion.1), kind=kOutput, calls=%fused_computation | convolution fusion | flops 537919488 | bytes 5767168 | tf_op jit(solution)/shard_map/thc,hcd->thd/dot_general | solution.py:395
  165.1 1.0 copy.23
  166.1 0.0 copy-done.4
  166.1 0.8 copy.51
  (1 shorter events, 0.0 us)
Async XLA Ops:
  3.4 61.7 %copy-start.6 = (f32[128,2]{0,1:T(2,128)S(1)}, f32[128,2]{0,1:T(2,128)}, u32[]{:S(2)}) copy-start(f32[128,2]{0,1:T(2,128)} %param.12) | copy-start | bytes 3076
  3.4 61.7 %copy-start.1 = (bf16[128,2048]{1,0:T(8,128)(2,1)S(1)}, bf16[128,2048]{1,0:T(8,128)(2,1)}, u32[]{:S(2)}) copy-start(bf16[128,2048]{1,0:T(8,128)(2,1)} %refs_4_.3) | copy-start | bytes 1572868
  63.1 4.5 %copy-start = (bf16[128,2048]{1,0:T(8,128)(2,1)S(1)}, bf16[128,2048]{1,0:T(8,128)(2,1)}, u32[]{:S(2)}) copy-start(bf16[128,2048]{1,0:T(8,128)(2,1)} %refs_3_.3) | copy-start | bytes 1572868
  63.1 4.5 %copy-start.2 = (bf16[32,64,512]{2,1,0:T(8,128)(2,1)S(1)}, bf16[32,64,512]{2,1,0:T(8,128)(2,1)}, u32[]{:S(2)}) copy-start(bf16[32,64,512]{2,1,0:T(8,128)(2,1)} %get-tuple-element.12) | copy-start | bytes 6291460
  67.6 1.6 copy-start.5
  71.0 87.9 %copy-start.3 = (bf16[128,2048]{1,0:T(8,128)(2,1)S(1)}, bf16[128,2048]{1,0:T(8,128)(2,1)}, u32[]{:S(2)}) copy-start(bf16[128,2048]{1,0:T(8,128)(2,1)} %refs_3_.2) | copy-start | bytes 1572868
  161.5 4.6 %copy-start.4 = (bf16[128,2048]{1,0:T(8,128)(2,1)S(1)}, bf16[128,2048]{1,0:T(8,128)(2,1)}, u32[]{:S(2)}) copy-start(bf16[128,2048]{1,0:T(8,128)(2,1)} %get-tuple-element.23) | copy-start | bytes 1572868
where the time goes:
time: 168 us; the launch traced here: 167 us
  Pallas kernels  144 us (86%)
  matrix products  11.2 us (7%)
  local copies, waits for them, and re-layouts  11 us (7%)
    pallas_call x1, Pallas kernels, update_weights(): pl.pallas_call(functools.partial(update_kernel, count), out_shape=[jax.Sh...  87.8 us
    pallas_call x1, Pallas kernels, gather_weights(): pl.pallas_call(functools.partial(gather_kernel, count), out_shape=[jax.Sh...  56 us
    dot_general x3, matrix products, project(): jnp.einsum('thd,hdc->thc', rows, matrix, preferred_element_type=jnp.float32)  5.35 us
    unnamed x19, local copies, waits for them, and re-layouts  4.67 us
    dot_general x1, matrix products, per_device(): jnp.einsum('thc,hcd->thd', mixed, new_two, preferred_element_type=jnp.flo...  3.6 us
    dynamic_slice x3, local copies, waits for them, and re-layouts, per_device(): lax.dynamic_slice(fulls[m].reshape(FAST_HEADS, FAST_DIM, FAST_HID), (star...  3.4 us

commit v1 on v0

v1 whole, which is shorter than its diff:
```python
import functools
import math

import jax
import jax.numpy as jnp
from jax import lax
from jax.experimental import pallas as pl
from jax.experimental.pallas import tpu as pltpu
from jax.sharding import PartitionSpec as P

ATT_HEADS = 16
FAST_HEADS = 2
WINDOW = 128
EPS = 1e-06

ONE, THREE, TWO = 0, 1, 2


def device(line, x, y, core):
    return ((line * 2 + y) * 2 + x) * 2 + core


def in_role(line, a, b, role):
    return device(line, a + role * (b - a), b + role * (a - b), role)


def bit_of(index, bit):
    return lax.rem(lax.div(index, jnp.int32(1 << bit)), jnp.int32(2))


def flipped(index, bit):
    return index + (1 - 2 * bit_of(index, bit)) * (1 << bit)


def remote(src, dst, send_sem, recv_sem, partner):
    return pltpu.make_async_remote_copy(
        src_ref=src,
        dst_ref=dst,
        send_sem=send_sem,
        recv_sem=recv_sem,
        device_id={"tok": partner},
        device_id_type=pl.DeviceIdType.MESH,
    )


def turned(row, size):
    return jnp.transpose(jnp.broadcast_to(row, (size, size)))


def nt_dot(left, right):
    return lax.dot_general(
        left, right, (((1,), (1,)), ((), ())), preferred_element_type=jnp.float32
    )


def dot(left, right):
    return jnp.dot(left, right, preferred_element_type=jnp.float32)


def flat(blocks):
    n, unit, width = blocks.shape
    if unit % 16 == 0:
        return blocks.reshape(n * unit, width)
    return blocks.astype(jnp.float32).reshape(n * unit, width).astype(jnp.bfloat16)


def kernel(count, *refs):
    w_refs = refs[:3]
    q_ref, k_ref, v_ref, seg_ref, rate_ref = refs[3:8]
    att_ref, out_ref = refs[8:10]
    (
        wbuf, kbuf, vbuf, qbuf, rbuf, rsend, asum, hid, total, staged, landed, old_own, old_all, new,
        z_own, z_peer, z_send, o_send, old_k, old_v, old_seg,
        first_s, first_r, first_l, mirror_s, mirror_r, mate_s, mate_r, side_s, side_r,
        tok_s, tok_r, sum_s, sum_r, all_s, all_r, end_s, end_r, halo_s, halo_r,
    ) = refs[10:]

    lines = count // 8
    half = lines // 2
    line_bits = lines.bit_length() - 1
    steps = line_bits + 1
    rows, hidden = w_refs[0].shape
    cols = hidden // 2
    tokens, width = q_ref.shape
    feats = width // FAST_HEADS
    blocks = 2 * lines
    unit = cols // blocks

    me = lax.axis_index("tok")
    core, chip = lax.rem(me, 2), lax.div(me, 2)
    x, y, line = lax.rem(chip, 2), lax.rem(lax.div(chip, 2), 2), lax.div(chip, 4)
    a, b = x + core * (y - x), y + core * (x - y)
    a_other, b_other = b, a
    other = 1 - core
    partner = device(line, x, y, other)
    pair = in_role(line, 1 - a, b, core)
    side = in_role(line, a, 1 - b, core)
    pair_sends = pair + other - core
    pair_takes = in_role(line, 1 - a_other, b_other, other)
    mirror_line = lax.rem(line + half, lines)
    mirror = in_role(mirror_line, a, b, core)
    upper = lax.div(line, half)
    place = line - upper * half
    base = upper * half

    def mate(i):
        return in_role(base + lax.rem(place + i, half), a, b, core)

    after, before = lax.rem(me + 1, count), lax.rem(me + count - 1, count)

    for group in range(FAST_HEADS):
        column = jnp.broadcast_to(rate_ref[:, group : group + 1], (tokens, tokens))
        rsend[group] = jnp.transpose(column)[0:8, :]

    barrier = pltpu.get_barrier_semaphore()
    known = [partner, pair, side, pair_sends, pair_takes, mirror, after, before]
    known += [mate(i) for i in range(1, half)]
    for one in known:
        pl.semaphore_signal(
            barrier, inc=1, device_id={"tok": one}, device_id_type=pl.DeviceIdType.MESH
        )
    pl.semaphore_wait(barrier, len(known))

    started = []

    def go(copy):
        copy.start()
        started.append(copy)

    head = upper
    head_a, head_b = x + head * (y - x), y + head * (x - y)
    stored = place * 4 + y * 2 + x

    def first(m, copy_half, kind):
        lanes = pl.ds(pl.multiple_of(copy_half * cols, cols), cols)
        src = w_refs[m].at[:, lanes]
        dst = wbuf.at[m, stored, pl.ds(pl.multiple_of(core * rows, rows), rows), :]
        if kind == "here":
            return pltpu.make_async_copy(src, dst, first_l.at[m])
        if kind == "core":
            return remote(src, dst, first_s.at[m, 0], first_r.at[m, 0], device(line, x, y, head))
        to = in_role(line, 1 - head_a, head_b, head)
        return remote(src, dst, first_s.at[m, 1], first_r.at[m, 1 + core], to)

    for m in range(3):
        go(first(m, 1 - head_a, "pair"))

        @pl.when(core == head)
        def _():
            first(m, head_a, "here").start()

        @pl.when(core != head)
        def _():
            first(m, head_a, "core").start()

    def own_lanes(group):
        return pl.ds(pl.multiple_of(group * feats, feats), feats)

    def send_tokens(kind):
        ref, buf = ((k_ref, kbuf), (v_ref, vbuf), (q_ref, qbuf), (rsend, rbuf))[kind]
        if kind == 3:
            mine, theirs = ref.at[core], ref.at[other]
        else:
            mine, theirs = ref.at[:, own_lanes(core)], ref.at[:, own_lanes(other)]
        here, there = buf.at[a * 2 + core], buf.at[a_other * 2 + core]
        go(remote(mine, here, tok_s.at[kind, 0], tok_r.at[kind, 1 + core], pair))
        go(remote(theirs, there, tok_s.at[kind, 1], tok_r.at[kind, 0], partner))
        go(remote(theirs, there, tok_s.at[kind, 2], tok_r.at[kind, 1 + core], pair_takes))
        if kind == 3:
            rbuf[a * 2 + core] = rsend[core]
        else:
            buf[a * 2 + core] = ref[:, own_lanes(core)]

    def take_tokens(kind):
        buf = (kbuf, vbuf, qbuf, rbuf)[kind]
        for i, slot in ((0, a * 2 + other), (1, (1 - a) * 2), (2, (1 - a) * 2 + 1)):
            ref = buf.at[slot]
            remote(ref, ref, tok_s.at[kind, i], tok_r.at[kind, i], partner).wait_recv()

    send_tokens(0)
    send_tokens(3)
    send_tokens(1)

    def piece(m, k, a_from, b_from):
        return wbuf.at[m, k * 4 + b_from * 2 + a_from + core * (a_from - b_from)]

    def first_wait(m):
        def part(a_from, c):
            ref = wbuf.at[m, place * 4 + b * 2 + a_from + core * (a_from - b)]
            return ref.at[pl.ds(pl.multiple_of(c * rows, rows), rows), :]

        first(m, head_a, "here").wait()
        ref = part(a, other)
        remote(ref, ref, first_s.at[m, 0], first_r.at[m, 0], partner).wait_recv()
        for c in range(2):
            ref = part(1 - a, c)
            remote(ref, ref, first_s.at[m, 1], first_r.at[m, 1 + c], pair).wait_recv()

    def to_mirror(m, i):
        ref = piece(m, place, i, b)
        return remote(ref, ref, mirror_s.at[m, i], mirror_r.at[m, i], mirror)

    def to_mate(m, i, step):
        ref = piece(m, place, i, b)
        return remote(ref, ref, mate_s.at[m, i, step], mate_r.at[m, i, step], mate(step))

    def from_mate(m, i, step):
        ref = piece(m, lax.rem(place + half - step, half), i, b)
        return remote(ref, ref, mate_s.at[m, i, step], mate_r.at[m, i, step], mate(step))

    def to_side(m, i, step):
        ref = piece(m, lax.rem(place + half - step, half), i, b)
        return remote(ref, ref, side_s.at[m, i, step], side_r.at[m, i, step], side)

    def from_side(m, i, step):
        ref = piece(m, lax.rem(place + half - step, half), i, 1 - b)
        return remote(ref, ref, side_s.at[m, i, step], side_r.at[m, i, step], side)

    for m in range(3):

        @pl.when(core == head)
        def _():
            first_wait(m)
            for i in range(2):
                to_mirror(m, i).start()

        @pl.when(core != head)
        def _():
            for i in range(2):
                to_mirror(m, i).wait_recv()

        for i in range(2):
            for step in range(1, half):
                go(to_mate(m, i, step))
            go(to_side(m, i, 0))
    for m in range(3):
        for step in range(1, half):
            for i in range(2):
                from_mate(m, i, step).wait_recv()
                go(to_side(m, i, step))

    def weight_there(m):
        for step in range(half):
            for i in range(2):
                from_side(m, i, step).wait_recv()

    def weight(m):
        return wbuf[m].reshape(feats, cols)

    all_keys = lambda: kbuf[...].reshape(4 * tokens, feats)
    all_values = lambda: vbuf[...].reshape(4 * tokens, feats)

    take_tokens(0)
    take_tokens(3)
    for m in (ONE, THREE):
        weight_there(m)
        asum[m] = dot(all_keys(), weight(m)).reshape(4, tokens, cols)

    def spread(s):
        column = turned(rbuf[s][0:1, :], tokens)
        return jnp.concatenate([column] * (cols // tokens), axis=1)

    def keep(m, s, value):
        lanes = pl.ds(pl.multiple_of(s * tokens, tokens), tokens)
        hid[m, :, lanes] = jnp.transpose(value).astype(jnp.bfloat16)

    def weigh(s, carry):
        a_one, a_three = asum[ONE, s], asum[THREE, s]
        keep(TWO, s, -spread(s) * a_one * jax.nn.sigmoid(a_one) * a_three)
        return carry

    lax.fori_loop(0, 4, weigh, 0)
    take_tokens(1)

    line_bit = [bit_of(line, i) for i in range(line_bits)]
    starts = [jnp.int32(0)]
    for i in range(line_bits):
        starts.append(starts[-1] + line_bit[i] * (lines >> (i + 1)))
    pos = b * lines + starts[-1]

    def gradient(m, which):
        at = pl.ds(pl.multiple_of(which * (cols // 2), cols // 2), cols // 2)
        grad = dot(hid[m, at, :], all_values() if m == TWO else all_keys())
        return grad.reshape(lines, unit, feats)

    def offset(step):
        return blocks - 2 * (lines >> step)

    def send_sum(m, step):
        at = pl.ds(offset(step), lines >> step)
        to = side if step == 0 else in_role(flipped(line, step - 1), a, b, core)
        return remote(
            staged.at[m, at], landed.at[m, at], sum_s.at[m, step], sum_r.at[m, step], to
        )

    def send_away(m):
        staged[m, pl.ds(0, lines)] = gradient(m, 1 - b).astype(jnp.bfloat16)
        go(send_sum(m, 0))

    def keep_own(m):
        total[m] = gradient(m, b)

    send_away(TWO)
    weight_there(TWO)
    asum[TWO] = dot(all_values(), weight(TWO)).reshape(4, tokens, cols)

    def deltas(s, carry):
        a_one, a_three = asum[ONE, s], asum[THREE, s]
        back = -spread(s) * asum[TWO, s]
        sig = jax.nn.sigmoid(a_one)
        keep(ONE, s, back * a_three * sig * (1.0 + a_one * (1.0 - sig)))
        keep(THREE, s, back * a_one * sig)
        return carry

    lax.fori_loop(0, 4, deltas, 0)
    send_away(ONE)
    send_away(THREE)
    send_tokens(2)
    halo = [
        remote(src, dst, halo_s.at[i], halo_r.at[i], after)
        for i, (src, dst) in enumerate(((seg_ref, old_seg), (k_ref, old_k), (v_ref, old_v)))
    ]

    @pl.when(me != count - 1)
    def _():
        for copy in halo:
            copy.start()

    @pl.when(me == 0)
    def _():
        old_k[...] = jnp.zeros_like(old_k)
        old_v[...] = jnp.zeros_like(old_v)
        old_seg[...] = jnp.zeros_like(old_seg)

    order = (TWO, ONE, THREE)
    for m in order:
        keep_own(m)
    for m in order:
        lanes = pl.ds(pl.multiple_of(b * (cols // 2), cols // 2), cols // 2)
        mine = wbuf[m, :, :, lanes].reshape(feats, cols // 2).astype(jnp.float32)
        old_all[...] = jnp.transpose(mine).reshape(lines, unit, feats)
        old_own[m] = old_all[starts[-1]]
    for step in range(1, steps):
        size = lines >> step
        bit = line_bit[step - 1]
        kept, away = starts[step], starts[step - 1] + (1 - bit) * size
        shift = offset(step - 1) - starts[step - 1]
        for m in order:
            send_sum(m, step - 1).wait_recv()

            def stage(i, carry):
                value = total[m, away + i] + landed[m, shift + away + i].astype(jnp.float32)
                staged[m, offset(step) + i] = value.astype(jnp.bfloat16)
                return carry

            def hold(i, carry):
                value = total[m, kept + i] + landed[m, shift + kept + i].astype(jnp.float32)
                total[m, kept + i] = value
                return carry

            lax.fori_loop(0, size, stage, 0)
            go(send_sum(m, step))
            lax.fori_loop(0, size, hold, 0)

    def span(part, position):
        if part == 0:
            return pl.ds(position, 1)
        size = 1 << (part - 1)
        return pl.ds(flipped(lax.div(position, jnp.int32(size)), 0) * size, size)

    def send_new(m, step, part):
        src = new.at[m, 0, span(part, pos)]
        if step == steps:
            dst, to = new.at[m, 1, span(part, pos)], pair
        elif step == steps - 1:
            dst, to = src, side
        else:
            dst, to = src, in_role(flipped(line, line_bits - 1 - step), a, b, core)
        return remote(src, dst, all_s.at[m, step, part], all_r.at[m, step, part], to)

    def new_there(m, step, part):
        if step == steps:
            ref = new.at[m, 1, span(part, pos)]
        else:
            ref = new.at[m, 0, span(part, flipped(pos, step))]
        return remote(ref, ref, all_s.at[m, step, part], all_r.at[m, step, part], side)

    def last_step(m):
        return steps + 1 if m == TWO else steps

    for m in order:
        send_sum(m, steps - 1).wait_recv()
        grad = total[m, starts[-1]] + landed[m, offset(steps - 1)].astype(jnp.float32)
        old = old_own[m]
        update = old - grad
        old_len = jnp.sqrt(jnp.sum(old * old, axis=1, keepdims=True))
        new_len = jnp.sqrt(jnp.sum(update * update, axis=1, keepdims=True) + EPS)
        new[m, 0, pos] = (update * (old_len / new_len)).astype(jnp.bfloat16)
        for step in range(last_step(m)):
            go(send_new(m, step, 0))

    dim = width // ATT_HEADS
    scale = 1.0 / math.sqrt(dim)

    @pl.when(me != 0)
    def _():
        for copy in halo:
            copy.wait_recv()

    def attend(first_head, last_head):
        row = lax.broadcasted_iota(jnp.int32, (tokens, tokens), 0)
        col = lax.broadcasted_iota(jnp.int32, (tokens, tokens), 1)
        seg_row = seg_ref[...].astype(jnp.float32)
        seg_col = turned(seg_row, tokens)
        now_ok = (col <= row) & (row - col < WINDOW) & (seg_col == seg_row)
        old_ok = (
            (row - col + tokens < WINDOW)
            & (seg_col == old_seg[...].astype(jnp.float32))
            & (row + me * tokens >= row + tokens)
        )

        def one(i, carry):
            lanes = pl.ds(pl.multiple_of(i * dim, dim), dim)
            q = q_ref[:, lanes]

            def score(keys, allowed):
                return jnp.where(allowed, nt_dot(q, keys) * scale, jnp.float32(-1e30))

            old, now = score(old_k[:, lanes], old_ok), score(k_ref[:, lanes], now_ok)
            top = jnp.maximum(
                jnp.max(old, axis=1, keepdims=True), jnp.max(now, axis=1, keepdims=True)
            )
            old = jnp.where(old_ok, jnp.exp(old - top), jnp.float32(0.0))
            now = jnp.where(now_ok, jnp.exp(now - top), jnp.float32(0.0))
            norm = jnp.sum(old, axis=1, keepdims=True) + jnp.sum(now, axis=1, keepdims=True)
            out = dot((old / norm).astype(jnp.bfloat16), old_v[:, lanes]) + dot(
                (now / norm).astype(jnp.bfloat16), v_ref[:, lanes]
            )
            att_ref[:, lanes] = out.astype(jnp.bfloat16)
            return carry

        lax.fori_loop(first_head, last_head, one, 0)

    for step in range(steps):
        for m in order:
            for part in range(step + 1):
                new_there(m, step, part).wait_recv()
            for later in range(step + 1, last_step(m)):
                go(send_new(m, later, step + 1))
        attend(ATT_HEADS * step // steps, ATT_HEADS * (step + 1) // steps)

    take_tokens(2)

    def mixed(place_from):
        rows_q = qbuf[pl.ds(place_from * 2, 2)].reshape(2 * tokens, feats)
        b_one = nt_dot(rows_q, flat(new[ONE, 0]))
        b_three = nt_dot(rows_q, flat(new[THREE, 0]))
        return (jax.nn.silu(b_one) * b_three).astype(jnp.bfloat16)

    z_send[...] = mixed(1 - a)
    z_copy = remote(z_send, z_peer, end_s.at[0], end_r.at[0], pair)
    go(z_copy)
    z_own[...] = mixed(a)
    for part in range(steps + 1):
        new_there(TWO, steps, part).wait_recv()
    z_copy.wait_recv()

    def fast_rows(c):
        at = pl.ds(pl.multiple_of(c * tokens, tokens), tokens)
        value = dot(z_own[at, :], flat(new[TWO, 0])) + dot(z_peer[at, :], flat(new[TWO, 1]))
        return value.astype(jnp.bfloat16)

    o_send[...] = fast_rows(other)
    out_copy = remote(
        o_send, out_ref.at[:, own_lanes(core)], end_s.at[1], end_r.at[1], partner
    )
    go(out_copy)
    out_ref[:, own_lanes(core)] = fast_rows(core)
    theirs = out_ref.at[:, own_lanes(other)]
    remote(theirs, theirs, end_s.at[1], end_r.at[1], partner).wait_recv()

    for copy in started:
        copy.wait_send()
    for m in range(3):

        @pl.when(core == head)
        def _():
            for i in range(2):
                to_mirror(m, i).wait_send()

        @pl.when(core != head)
        def _():
            first(m, head_a, "core").wait_send()

    @pl.when(me != count - 1)
    def _():
        for copy in halo:
            copy.wait_send()


def per_device(queries, keys, values, segment, rates, fast_one, fast_three, fast_two):
    count = lax.axis_size("tok")
    tokens, width = queries.shape
    rows, hidden = fast_one.shape
    lines = count // 8
    half = lines // 2
    steps = lines.bit_length()
    feats = width // FAST_HEADS
    cols = hidden // 2
    blocks = 2 * lines
    unit = cols // blocks
    bf16, f32 = jnp.bfloat16, jnp.float32
    dma = pltpu.SemaphoreType.DMA
    return pl.pallas_call(
        functools.partial(kernel, count),
        out_shape=[jax.ShapeDtypeStruct(queries.shape, bf16)] * 2,
        in_specs=[pl.BlockSpec(memory_space=pltpu.VMEM)] * 8,
        out_specs=[pl.BlockSpec(memory_space=pltpu.VMEM)] * 2,
        scratch_shapes=[
            pltpu.VMEM((3, count // 4, 2 * rows, cols), bf16),
            pltpu.VMEM((4, tokens, feats), bf16),
            pltpu.VMEM((4, tokens, feats), bf16),
            pltpu.VMEM((4, tokens, feats), bf16),
            pltpu.VMEM((4, 8, tokens), f32),
            pltpu.VMEM((FAST_HEADS, 8, tokens), f32),
            pltpu.VMEM((3, 4, tokens, cols), f32),
            pltpu.VMEM((3, cols, 4 * tokens), bf16),
            pltpu.VMEM((3, lines, unit, feats), f32),
            pltpu.VMEM((3, blocks, unit, feats), bf16),
            pltpu.VMEM((3, blocks, unit, feats), bf16),
            pltpu.VMEM((3, unit, feats), f32),
            pltpu.VMEM((lines, unit, feats), f32),
            pltpu.VMEM((3, 2, blocks, unit, feats), bf16),
            pltpu.VMEM((2 * tokens, cols), bf16),
            pltpu.VMEM((2 * tokens, cols), bf16),
            pltpu.VMEM((2 * tokens, cols), bf16),
            pltpu.VMEM((tokens, feats), bf16),
            pltpu.VMEM(keys.shape, bf16),
            pltpu.VMEM(values.shape, bf16),
            pltpu.VMEM((1, tokens), jnp.int32),
            dma((3, 2)),
            dma((3, 3)),
            dma((3,)),
            dma((3, 2)),
            dma((3, 2)),
            dma((3, 2, half)),
            dma((3, 2, half)),
            dma((3, 2, half)),
            dma((3, 2, half)),
            dma((4, 3)),
            dma((4, 3)),
            dma((3, steps)),
            dma((3, steps)),
            dma((3, steps + 1, steps + 1)),
            dma((3, steps + 1, steps + 1)),
            dma((2,)),
            dma((2,)),
            dma((3,)),
            dma((3,)),
        ],
        compiler_params=pltpu.CompilerParams(collective_id=0, has_side_effects=True),
    )(
        fast_one, fast_three, fast_two, queries, keys, values, segment.reshape(1, tokens), rates
    )


def solution(mesh):
    placed = P(("grp", "tok"), None)
    return jax.shard_map(
        per_device,
        mesh=mesh,
        in_specs=(placed, placed, placed, P(("grp", "tok")), placed, placed, placed, placed),
        out_specs=(placed, placed),
        check_vma=False,
    )
```

time: 168 us -> 95.7 us (0.57)
  the two profiles are of different devices: /device:TPU:1 before, /device:TPU:3 now
where the time goes in v1:
time: 95.7 us; the launch traced here: 95.5 us
  Pallas kernels  90.7 us (95%)
  local copies, waits for them, and re-layouts  4.15 us (4%)
    pallas_call x1, Pallas kernels, per_device(): pl.pallas_call(functools.partial(kernel, count), out_shape=[jax.ShapeDtyp...  90.7 us
    unnamed x7, local copies, waits for them, and re-layouts  4.15 us

profile of v1, /device:TPU:3, one launch (start us, length us, event | category | flops | bytes accessed | tf_op | source)
XLA Modules:
  0.0 95.5 jit_solution(14012307856753235290)
XLA Ops:
  0.6 0.0 copy-start.1
  0.6 0.7 copy-done.1
  1.3 0.7 copy.10.refs_7_
  2.0 90.7 %shard_map.95 = (bf16[128,2048]{1,0:T(8,128)(2,1)}, bf16[128,2048]{1,0:T(8,128)(2,1)}) custom-call(bf16[64,512]{1,0:T(8,128)(2,1)} %refs_0_.1, bf16[64,512]{1,0:T(8,128)(2,1)} %refs_1_.1, bf16[64,512]{1,0:T(8,128)(2,1)} %refs_2_.1, bf16[128,2048]{1,0:T(8,128)(2,1)} %refs_3_.1, bf16[128,2048]{1,0:T(8,128)(2,1)} %refs_4_.1, bf16[128,2048]{1,0:T(8,128)(2,1)} %refs_5_.1, ...), custom_call_target="tpu_custom_call" | custom-call | tf_op jit(solution)/shard_map/pallas_call | solution.py:514
  92.7 0.0 copy-start
  92.7 1.9 %copy.13 = bf16[128,2048]{1,0:T(8,128)(2,1)} copy(bf16[128,2048]{1,0:T(8,128)(2,1)} %get-tuple-element.4) | data formatting | bytes 1048576
  94.7 0.0 copy-done
  94.7 0.8 copy.14
Async XLA Ops:
  0.6 0.7 copy-start.1
  92.7 2.0 %copy-start = (bf16[128,2048]{1,0:T(8,128)(2,1)S(1)}, bf16[128,2048]{1,0:T(8,128)(2,1)}, u32[]{:S(2)}) copy-start(bf16[128,2048]{1,0:T(8,128)(2,1)} %get-tuple-element.5) | copy-start | bytes 1572868

commit v2 on v1

--- a/solution.py
+++ b/solution.py
@@ -14,6 +14,7 @@
 EPS = 1e-06
 
 ONE, THREE, TWO = 0, 1, 2
+WIDE = ()
 
 
 def device(line, x, y, core):
@@ -95,7 +96,6 @@
     partner = device(line, x, y, other)
     pair = in_role(line, 1 - a, b, core)
     side = in_role(line, a, 1 - b, core)
-    pair_sends = pair + other - core
     pair_takes = in_role(line, 1 - a_other, b_other, other)
     mirror_line = lax.rem(line + half, lines)
     mirror = in_role(mirror_line, a, b, core)
@@ -109,12 +109,12 @@
     after, before = lax.rem(me + 1, count), lax.rem(me + count - 1, count)
 
     for group in range(FAST_HEADS):
-        column = jnp.broadcast_to(rate_ref[:, group : group + 1], (tokens, tokens))
-        rsend[group] = jnp.transpose(column)[0:8, :]
+        rsend[group] = jnp.broadcast_to(rate_ref[group : group + 1, :], (8, tokens))
 
     barrier = pltpu.get_barrier_semaphore()
-    known = [partner, pair, side, pair_sends, pair_takes, mirror, after, before]
-    known += [mate(i) for i in range(1, half)]
+    plane = line * 8
+    known = [plane + lax.rem(me - plane + i, 8) for i in range(1, 8)]
+    known += [mirror, after, before] + [mate(i) for i in range(1, half)]
     for one in known:
         pl.semaphore_signal(
             barrier, inc=1, device_id={"tok": one}, device_id_type=pl.DeviceIdType.MESH
@@ -131,27 +131,34 @@
     head_a, head_b = x + head * (y - x), y + head * (x - y)
     stored = place * 4 + y * 2 + x
 
-    def first(m, copy_half, kind):
-        lanes = pl.ds(pl.multiple_of(copy_half * cols, cols), cols)
-        src = w_refs[m].at[:, lanes]
+    def first(m, far):
+        cross, apart = far % 2, far // 2
+        start = (head_a + cross - 2 * cross * head_a) * cols
+        src = w_refs[m].at[:, pl.ds(pl.multiple_of(start, cols), cols)]
         dst = wbuf.at[m, stored, pl.ds(pl.multiple_of(core * rows, rows), rows), :]
-        if kind == "here":
-            return pltpu.make_async_copy(src, dst, first_l.at[m])
-        if kind == "core":
-            return remote(src, dst, first_s.at[m, 0], first_r.at[m, 0], device(line, x, y, head))
-        to = in_role(line, 1 - head_a, head_b, head)
-        return remote(src, dst, first_s.at[m, 1], first_r.at[m, 1 + core], to)
+        to_a = 1 - head_a if cross else head_a
+        to = in_role(line, to_a, 1 - head_b if apart else head_b, head)
+        return remote(src, dst, first_s.at[m, far], first_r.at[m, far, core], to)
+
+    def first_here(m):
+        src = w_refs[m].at[:, pl.ds(pl.multiple_of(head_a * cols, cols), cols)]
+        dst = wbuf.at[m, stored, pl.ds(pl.multiple_of(core * rows, rows), rows), :]
+        return pltpu.make_async_copy(src, dst, first_l.at[m])
+
+    def reach(m):
+        return 4 if m in WIDE else 2
 
     for m in range(3):
-        go(first(m, 1 - head_a, "pair"))
+        for far in range(1, reach(m)):
+            go(first(m, far))
 
         @pl.when(core == head)
         def _():
-            first(m, head_a, "here").start()
+            first_here(m).start()
 
         @pl.when(core != head)
         def _():
-            first(m, head_a, "core").start()
+            first(m, 0).start()
 
     def own_lanes(group):
         return pl.ds(pl.multiple_of(group * feats, feats), feats)
@@ -181,20 +188,24 @@
     send_tokens(3)
     send_tokens(1)
 
-    def piece(m, k, a_from, b_from):
-        return wbuf.at[m, k * 4 + b_from * 2 + a_from + core * (a_from - b_from)]
+    def pairs(m):
+        return 1 if m in WIDE else 2
+
+    def piece(m, k, i, b_from):
+        if m in WIDE:
+            return wbuf.at[m, pl.ds(k * 4, 4)]
+        return wbuf.at[m, k * 4 + b_from * 2 + i + core * (i - b_from)]
 
     def first_wait(m):
-        def part(a_from, c):
-            ref = wbuf.at[m, place * 4 + b * 2 + a_from + core * (a_from - b)]
-            return ref.at[pl.ds(pl.multiple_of(c * rows, rows), rows), :]
-
-        first(m, head_a, "here").wait()
-        ref = part(a, other)
-        remote(ref, ref, first_s.at[m, 0], first_r.at[m, 0], partner).wait_recv()
-        for c in range(2):
-            ref = part(1 - a, c)
-            remote(ref, ref, first_s.at[m, 1], first_r.at[m, 1 + c], pair).wait_recv()
+        first_here(m).wait()
+        for far in range(reach(m)):
+            from_a = 1 - a if far % 2 else a
+            from_b = 1 - b if far // 2 else b
+            block = wbuf.at[m, place * 4 + from_b * 2 + from_a + core * (from_a - from_b)]
+            for c in (other,) if far == 0 else (0, 1):
+                ref = block.at[pl.ds(pl.multiple_of(c * rows, rows), rows), :]
+                copy = remote(ref, ref, first_s.at[m, far], first_r.at[m, far, c], partner)
+                copy.wait_recv()
 
     def to_mirror(m, i):
         ref = piece(m, place, i, b)
@@ -221,25 +232,32 @@
         @pl.when(core == head)
         def _():
             first_wait(m)
-            for i in range(2):
+            for i in range(pairs(m)):
                 to_mirror(m, i).start()
 
         @pl.when(core != head)
         def _():
-            for i in range(2):
+            for i in range(pairs(m)):
                 to_mirror(m, i).wait_recv()
 
-        for i in range(2):
+        for i in range(pairs(m)):
             for step in range(1, half):
                 go(to_mate(m, i, step))
-            go(to_side(m, i, 0))
+            if m not in WIDE:
+                go(to_side(m, i, 0))
     for m in range(3):
+        if m in WIDE:
+            continue
         for step in range(1, half):
             for i in range(2):
                 from_mate(m, i, step).wait_recv()
                 go(to_side(m, i, step))
 
     def weight_there(m):
+        if m in WIDE:
+            for step in range(1, half):
+                from_mate(m, 0, step).wait_recv()
+            return
         for step in range(half):
             for i in range(2):
                 from_side(m, i, step).wait_recv()
@@ -249,12 +267,6 @@
 
     all_keys = lambda: kbuf[...].reshape(4 * tokens, feats)
     all_values = lambda: vbuf[...].reshape(4 * tokens, feats)
-
-    take_tokens(0)
-    take_tokens(3)
-    for m in (ONE, THREE):
-        weight_there(m)
-        asum[m] = dot(all_keys(), weight(m)).reshape(4, tokens, cols)
 
     def spread(s):
         column = turned(rbuf[s][0:1, :], tokens)
@@ -268,9 +280,6 @@
         a_one, a_three = asum[ONE, s], asum[THREE, s]
         keep(TWO, s, -spread(s) * a_one * jax.nn.sigmoid(a_one) * a_three)
         return carry
-
-    lax.fori_loop(0, 4, weigh, 0)
-    take_tokens(1)
 
     line_bit = [bit_of(line, i) for i in range(line_bits)]
     starts = [jnp.int32(0)]
@@ -300,9 +309,11 @@
     def keep_own(m):
         total[m] = gradient(m, b)
 
-    send_away(TWO)
-    weight_there(TWO)
-    asum[TWO] = dot(all_values(), weight(TWO)).reshape(4, tokens, cols)
+    def keep_old(m):
+        lanes = pl.ds(pl.multiple_of(b * (cols // 2), cols // 2), cols // 2)
+        mine = wbuf[m, :, :, lanes].reshape(feats, cols // 2).astype(jnp.float32)
+        old_all[...] = jnp.transpose(mine).reshape(lines, unit, feats)
+        old_own[m] = old_all[starts[-1]]
 
     def deltas(s, carry):
         a_one, a_three = asum[ONE, s], asum[THREE, s]
@@ -312,6 +323,22 @@
         keep(THREE, s, back * a_one * sig)
         return carry
 
+    def project(m):
+        weight_there(m)
+        rows_in = all_values() if m == TWO else all_keys()
+        asum[m] = dot(rows_in, weight(m)).reshape(4, tokens, cols)
+
+    take_tokens(0)
+    take_tokens(3)
+    project(ONE)
+    project(THREE)
+    lax.fori_loop(0, 4, weigh, 0)
+    take_tokens(1)
+    send_away(TWO)
+    keep_own(TWO)
+    keep_old(ONE)
+    keep_old(THREE)
+    project(TWO)
     lax.fori_loop(0, 4, deltas, 0)
     send_away(ONE)
     send_away(THREE)
@@ -333,34 +360,27 @@
         old_seg[...] = jnp.zeros_like(old_seg)
 
     order = (TWO, ONE, THREE)
-    for m in order:
-        keep_own(m)
-    for m in order:
-        lanes = pl.ds(pl.multiple_of(b * (cols // 2), cols // 2), cols // 2)
-        mine = wbuf[m, :, :, lanes].reshape(feats, cols // 2).astype(jnp.float32)
-        old_all[...] = jnp.transpose(mine).reshape(lines, unit, feats)
-        old_own[m] = old_all[starts[-1]]
-    for step in range(1, steps):
+
+    def pass_on(m, step):
         size = lines >> step
         bit = line_bit[step - 1]
         kept, away = starts[step], starts[step - 1] + (1 - bit) * size
         shift = offset(step - 1) - starts[step - 1]
-        for m in order:
-            send_sum(m, step - 1).wait_recv()
-
-            def stage(i, carry):
-                value = total[m, away + i] + landed[m, shift + away + i].astype(jnp.float32)
-                staged[m, offset(step) + i] = value.astype(jnp.bfloat16)
-                return carry
-
-            def hold(i, carry):
-                value = total[m, kept + i] + landed[m, shift + kept + i].astype(jnp.float32)
-                total[m, kept + i] = value
-                return carry
-
-            lax.fori_loop(0, size, stage, 0)
-            go(send_sum(m, step))
-            lax.fori_loop(0, size, hold, 0)
+        send_sum(m, step - 1).wait_recv()
+
+        def stage(i, carry):
+            value = total[m, away + i] + landed[m, shift + away + i].astype(jnp.float32)
+            staged[m, offset(step) + i] = value.astype(jnp.bfloat16)
+            return carry
+
+        def hold(i, carry):
+            value = total[m, kept + i] + landed[m, shift + kept + i].astype(jnp.float32)
+            total[m, kept + i] = value
+            return carry
+
+        lax.fori_loop(0, size, stage, 0)
+        go(send_sum(m, step))
+        lax.fori_loop(0, size, hold, 0)
 
     def span(part, position):
         if part == 0:
@@ -388,7 +408,7 @@
     def last_step(m):
         return steps + 1 if m == TWO else steps
 
-    for m in order:
+    def renew(m):
         send_sum(m, steps - 1).wait_recv()
         grad = total[m, starts[-1]] + landed[m, offset(steps - 1)].astype(jnp.float32)
         old = old_own[m]
@@ -398,6 +418,18 @@
         new[m, 0, pos] = (update * (old_len / new_len)).astype(jnp.bfloat16)
         for step in range(last_step(m)):
             go(send_new(m, step, 0))
+
+    pass_on(TWO, 1)
+    keep_own(ONE)
+    pass_on(ONE, 1)
+    keep_own(THREE)
+    pass_on(THREE, 1)
+    keep_old(TWO)
+    for step in range(2, steps):
+        for m in order:
+            pass_on(m, step)
+    for m in order:
+        renew(m)
 
     dim = width // ATT_HEADS
     scale = 1.0 / math.sqrt(dim)
@@ -441,21 +473,26 @@
 
         lax.fori_loop(first_head, last_head, one, 0)
 
-    for step in range(steps):
-        for m in order:
-            for part in range(step + 1):
-                new_there(m, step, part).wait_recv()
-            for later in range(step + 1, last_step(m)):
-                go(send_new(m, later, step + 1))
-        attend(ATT_HEADS * step // steps, ATT_HEADS * (step + 1) // steps)
-
-    take_tokens(2)
-
     def mixed(place_from):
-        rows_q = qbuf[pl.ds(place_from * 2, 2)].reshape(2 * tokens, feats)
-        b_one = nt_dot(rows_q, flat(new[ONE, 0]))
+        slots = pl.ds(place_from * 2, 2)
+        rows_q = qbuf[slots].reshape(2 * tokens, feats)
+        b_one = asum[ONE, slots].reshape(2 * tokens, cols)
         b_three = nt_dot(rows_q, flat(new[THREE, 0]))
         return (jax.nn.silu(b_one) * b_three).astype(jnp.bfloat16)
+
+    slots = len(order) * steps - 1
+    for slot, (step, m) in enumerate((step, m) for step in range(steps) for m in order):
+        for part in range(step + 1):
+            new_there(m, step, part).wait_recv()
+        for later in range(step + 1, last_step(m)):
+            go(send_new(m, later, step + 1))
+        if slot < slots:
+            attend(ATT_HEADS * slot // slots, ATT_HEADS * (slot + 1) // slots)
+        if (m, step) == (ONE, steps - 1):
+            take_tokens(2)
+            asum[ONE] = nt_dot(
+                qbuf[...].reshape(4 * tokens, feats), flat(new[ONE, 0])
+            ).reshape(4, tokens, cols)
 
     z_send[...] = mixed(1 - a)
     z_copy = remote(z_send, z_peer, end_s.at[0], end_r.at[0], pair)
@@ -485,12 +522,12 @@
 
         @pl.when(core == head)
         def _():
-            for i in range(2):
+            for i in range(pairs(m)):
                 to_mirror(m, i).wait_send()
 
         @pl.when(core != head)
         def _():
-            first(m, head_a, "core").wait_send()
+            first(m, 0).wait_send()
 
     @pl.when(me != count - 1)
     def _():
@@ -538,8 +575,8 @@
             pltpu.VMEM(keys.shape, bf16),
             pltpu.VMEM(values.shape, bf16),
             pltpu.VMEM((1, tokens), jnp.int32),
-            dma((3, 2)),
-            dma((3, 3)),
+            dma((3, 4)),
+            dma((3, 4, 2)),
             dma((3,)),
             dma((3, 2)),
             dma((3, 2)),
@@ -558,9 +595,11 @@
             dma((3,)),
             dma((3,)),
         ],
-        compiler_params=pltpu.CompilerParams(collective_id=0, has_side_effects=True),
+        compiler_params=pltpu.CompilerParams(
+            collective_id=0, has_side_effects=True
+        ),
     )(
-        fast_one, fast_three, fast_two, queries, keys, values, segment.reshape(1, tokens), rates
+        fast_one, fast_three, fast_two, queries, keys, values, segment.reshape(1, tokens), rates.T
     )
 
 

time: 95.7 us -> 90.4 us (0.945)
  the two profiles are of different devices: /device:TPU:3 before, /device:TPU:7 now
where the time goes in v2:
time: 90.4 us; the launch traced here: 90.2 us
  Pallas kernels  86.8 us (96%)
  local copies, waits for them, and re-layouts  2.74 us (3%)
    pallas_call x1, Pallas kernels, per_device(): pl.pallas_call(functools.partial(kernel, count), out_shape=[jax.ShapeDtyp...  86.8 us
    unnamed x4, local copies, waits for them, and re-layouts  2.74 us

profile of v2, /device:TPU:7, one launch (start us, length us, event | category | flops | bytes accessed | tf_op | source)
XLA Modules:
  0.0 90.2 jit_solution(14378312998953316800)
XLA Ops:
  0.6 86.8 %shard_map.95 = (bf16[128,2048]{1,0:T(8,128)(2,1)}, bf16[128,2048]{1,0:T(8,128)(2,1)}) custom-call(bf16[64,512]{1,0:T(8,128)(2,1)} %refs_0_.1, bf16[64,512]{1,0:T(8,128)(2,1)} %refs_1_.1, bf16[64,512]{1,0:T(8,128)(2,1)} %refs_2_.1, bf16[128,2048]{1,0:T(8,128)(2,1)} %refs_3_.1, bf16[128,2048]{1,0:T(8,128)(2,1)} %refs_4_.1, bf16[128,2048]{1,0:T(8,128)(2,1)} %refs_5_.1, ...), custom_call_target="tpu_custom_call" | custom-call | tf_op jit(solution)/shard_map/pallas_call | solution.py:551
  87.5 0.0 copy-start
  87.5 1.9 %copy.12 = bf16[128,2048]{1,0:T(8,128)(2,1)} copy(bf16[128,2048]{1,0:T(8,128)(2,1)} %get-tuple-element.4) | data formatting | bytes 1048576
  89.4 0.0 copy-done
  89.4 0.8 copy.13
Async XLA Ops:
  87.5 2.0 %copy-start = (bf16[128,2048]{1,0:T(8,128)(2,1)S(1)}, bf16[128,2048]{1,0:T(8,128)(2,1)}, u32[]{:S(2)}) copy-start(bf16[128,2048]{1,0:T(8,128)(2,1)} %get-tuple-element.5) | copy-start | bytes 1572868

commit v3 on v2

--- a/solution.py
+++ b/solution.py
@@ -14,7 +14,8 @@
 EPS = 1e-06
 
 ONE, THREE, TWO = 0, 1, 2
-WIDE = ()
+WIDE = (TWO,)
+SPLIT = 2
 
 
 def device(line, x, y, core):
@@ -66,15 +67,16 @@
 
 
 def kernel(count, *refs):
-    w_refs = refs[:3]
-    q_ref, k_ref, v_ref, seg_ref, rate_ref = refs[3:8]
     att_ref, out_ref = refs[8:10]
+    loaded, load_sem = refs[10:18], refs[18]
+    w_refs = loaded[:3]
+    q_ref, k_ref, v_ref, seg_ref, rate_ref = loaded[3:8]
     (
         wbuf, kbuf, vbuf, qbuf, rbuf, rsend, asum, hid, total, staged, landed, old_own, old_all, new,
         z_own, z_peer, z_send, o_send, old_k, old_v, old_seg,
         first_s, first_r, first_l, mirror_s, mirror_r, mate_s, mate_r, side_s, side_r,
         tok_s, tok_r, sum_s, sum_r, all_s, all_r, end_s, end_r, halo_s, halo_r,
-    ) = refs[10:]
+    ) = refs[19:]
 
     lines = count // 8
     half = lines // 2
@@ -86,6 +88,13 @@
     feats = width // FAST_HEADS
     blocks = 2 * lines
     unit = cols // blocks
+    wide = feats // SPLIT
+
+    def parts(m):
+        return range(m * SPLIT, (m + 1) * SPLIT)
+
+    def lanes_of(v):
+        return slice(v % SPLIT * wide, (v % SPLIT + 1) * wide)
 
     me = lax.axis_index("tok")
     core, chip = lax.rem(me, 2), lax.div(me, 2)
@@ -106,19 +115,28 @@
     def mate(i):
         return in_role(base + lax.rem(place + i, half), a, b, core)
 
-    after, before = lax.rem(me + 1, count), lax.rem(me + count - 1, count)
-
-    for group in range(FAST_HEADS):
-        rsend[group] = jnp.broadcast_to(rate_ref[group : group + 1, :], (8, tokens))
+    def around(i):
+        return lax.rem(me + count + i, count)
+
+    after = around(1)
+    loads = [pltpu.make_async_copy(refs[i], loaded[i], load_sem.at[i]) for i in range(8)]
+    loading = (0, 1, 2, 4, 7, 5, 6, 3)
+    for i in loading:
+        loads[i].start()
 
     barrier = pltpu.get_barrier_semaphore()
     plane = line * 8
     known = [plane + lax.rem(me - plane + i, 8) for i in range(1, 8)]
-    known += [mirror, after, before] + [mate(i) for i in range(1, half)]
+    known += [mirror] + [mate(i) for i in range(1, half)]
+    known += [around(i) for i in (1, -1, 4, -4, 5, -5)]
     for one in known:
         pl.semaphore_signal(
             barrier, inc=1, device_id={"tok": one}, device_id_type=pl.DeviceIdType.MESH
         )
+    for i in loading:
+        loads[i].wait()
+    for group in range(FAST_HEADS):
+        rsend[group] = jnp.broadcast_to(rate_ref[group : group + 1, :], (8, tokens))
     pl.semaphore_wait(barrier, len(known))
 
     started = []
@@ -268,18 +286,24 @@
     all_keys = lambda: kbuf[...].reshape(4 * tokens, feats)
     all_values = lambda: vbuf[...].reshape(4 * tokens, feats)
 
+    def part_of(which):
+        return pl.ds(pl.multiple_of(which * (cols // 2), cols // 2), cols // 2)
+
     def spread(s):
         column = turned(rbuf[s][0:1, :], tokens)
-        return jnp.concatenate([column] * (cols // tokens), axis=1)
-
-    def keep(m, s, value):
+        return jnp.concatenate([column] * (cols // 2 // tokens), axis=1)
+
+    def keep(m, s, which, value):
         lanes = pl.ds(pl.multiple_of(s * tokens, tokens), tokens)
-        hid[m, :, lanes] = jnp.transpose(value).astype(jnp.bfloat16)
-
-    def weigh(s, carry):
-        a_one, a_three = asum[ONE, s], asum[THREE, s]
-        keep(TWO, s, -spread(s) * a_one * jax.nn.sigmoid(a_one) * a_three)
-        return carry
+        hid[m, part_of(which), lanes] = jnp.transpose(value).astype(jnp.bfloat16)
+
+    def weigh(which):
+        def one(s, carry):
+            a_one, a_three = asum[ONE, s, :, part_of(which)], asum[THREE, s, :, part_of(which)]
+            keep(TWO, s, which, -spread(s) * a_one * jax.nn.sigmoid(a_one) * a_three)
+            return carry
+
+        lax.fori_loop(0, 4, one, 0)
 
     line_bit = [bit_of(line, i) for i in range(line_bits)]
     starts = [jnp.int32(0)]
@@ -287,10 +311,11 @@
         starts.append(starts[-1] + line_bit[i] * (lines >> (i + 1)))
     pos = b * lines + starts[-1]
 
-    def gradient(m, which):
-        at = pl.ds(pl.multiple_of(which * (cols // 2), cols // 2), cols // 2)
-        grad = dot(hid[m, at, :], all_values() if m == TWO else all_keys())
-        return grad.reshape(lines, unit, feats)
+    def gradient(v, which):
+        m = v // SPLIT
+        ref = vbuf if m == TWO else kbuf
+        side_rows = ref[:, :, lanes_of(v)].reshape(4 * tokens, wide)
+        return dot(hid[m, part_of(which), :], side_rows).reshape(lines, unit, wide)
 
     def offset(step):
         return blocks - 2 * (lines >> step)
@@ -303,11 +328,13 @@
         )
 
     def send_away(m):
-        staged[m, pl.ds(0, lines)] = gradient(m, 1 - b).astype(jnp.bfloat16)
-        go(send_sum(m, 0))
+        for v in parts(m):
+            staged[v, pl.ds(0, lines)] = gradient(v, 1 - b).astype(jnp.bfloat16)
+            go(send_sum(v, 0))
 
     def keep_own(m):
-        total[m] = gradient(m, b)
+        for v in parts(m):
+            total[v] = gradient(v, b)
 
     def keep_old(m):
         lanes = pl.ds(pl.multiple_of(b * (cols // 2), cols // 2), cols // 2)
@@ -315,13 +342,16 @@
         old_all[...] = jnp.transpose(mine).reshape(lines, unit, feats)
         old_own[m] = old_all[starts[-1]]
 
-    def deltas(s, carry):
-        a_one, a_three = asum[ONE, s], asum[THREE, s]
-        back = -spread(s) * asum[TWO, s]
-        sig = jax.nn.sigmoid(a_one)
-        keep(ONE, s, back * a_three * sig * (1.0 + a_one * (1.0 - sig)))
-        keep(THREE, s, back * a_one * sig)
-        return carry
+    def deltas(which):
+        def one(s, carry):
+            a_one, a_three = asum[ONE, s, :, part_of(which)], asum[THREE, s, :, part_of(which)]
+            back = -spread(s) * asum[TWO, s, :, part_of(which)]
+            sig = jax.nn.sigmoid(a_one)
+            keep(ONE, s, which, back * a_three * sig * (1.0 + a_one * (1.0 - sig)))
+            keep(THREE, s, which, back * a_one * sig)
+            return carry
+
+        lax.fori_loop(0, 4, one, 0)
 
     def project(m):
         weight_there(m)
@@ -332,32 +362,86 @@
     take_tokens(3)
     project(ONE)
     project(THREE)
-    lax.fori_loop(0, 4, weigh, 0)
+    weigh(1 - b)
     take_tokens(1)
     send_away(TWO)
+    weigh(b)
     keep_own(TWO)
     keep_old(ONE)
     keep_old(THREE)
     project(TWO)
-    lax.fori_loop(0, 4, deltas, 0)
+    deltas(1 - b)
     send_away(ONE)
     send_away(THREE)
     send_tokens(2)
-    halo = [
-        remote(src, dst, halo_s.at[i], halo_r.at[i], after)
-        for i, (src, dst) in enumerate(((seg_ref, old_seg), (k_ref, old_k), (v_ref, old_v)))
-    ]
-
-    @pl.when(me != count - 1)
-    def _():
-        for copy in halo:
-            copy.start()
+
+    seg_copy = remote(seg_ref, old_seg, halo_s.at[4], halo_r.at[4], after)
+    kinds = ((k_ref, kbuf, old_k), (v_ref, vbuf, old_v))
+
+    def halo(i, group):
+        ref, buf, old = kinds[i]
+        if group is None:
+            return remote(ref, old, halo_s.at[i], halo_r.at[i], partner)
+        at = old.at[:, pl.ds(group * feats, feats)]
+        if group == 0:
+            slot, to = 3, device(lax.rem(line + y, lines), 0, 1 - y, 0)
+        else:
+            slot = (y + x - 2 * x * y) * 2 + 1
+            to = device(lax.rem(line + x * (1 - y), lines), 1 - x, y, 0)
+        return remote(buf.at[slot], at, halo_s.at[i * 2 + group], halo_r.at[i * 2 + group], to)
+
+    def halo_from(i, group):
+        ref, buf, old = kinds[i]
+        if group is None:
+            return halo(i, None)
+        at = old.at[:, pl.ds(group * feats, feats)]
+        return remote(at, at, halo_s.at[i * 2 + group], halo_r.at[i * 2 + group], partner)
+
+    last_line = line == lines - 1
+    sends_zero = (core == 0) & (x == 0) & jnp.logical_not((y == 1) & last_line)
+    sends_one = (core == 1) & jnp.logical_not((x == 1) & (y == 0) & last_line)
+
+    def each_halo(act_inner, act_zero, act_one, act_seg, inner, zero, one, seg):
+        @pl.when(inner)
+        def _():
+            for i in range(2):
+                act_inner(i)
+
+        @pl.when(zero)
+        def _():
+            for i in range(2):
+                act_zero(i)
+
+        @pl.when(one)
+        def _():
+            for i in range(2):
+                act_one(i)
+
+        @pl.when(seg)
+        def _():
+            act_seg()
+
+    each_halo(
+        lambda i: halo(i, None).start(),
+        lambda i: halo(i, 0).start(),
+        lambda i: halo(i, 1).start(),
+        seg_copy.start,
+        core == 0,
+        sends_zero,
+        sends_one,
+        me != count - 1,
+    )
 
     @pl.when(me == 0)
     def _():
         old_k[...] = jnp.zeros_like(old_k)
         old_v[...] = jnp.zeros_like(old_v)
         old_seg[...] = jnp.zeros_like(old_seg)
+
+    @pl.when((core == 0) & (x == 1))
+    def _():
+        for _, buf, old in kinds:
+            old[:, 0:feats] = buf[1]
 
     order = (TWO, ONE, THREE)
 
@@ -381,6 +465,10 @@
         lax.fori_loop(0, size, stage, 0)
         go(send_sum(m, step))
         lax.fori_loop(0, size, hold, 0)
+
+    def pass_all(m, step):
+        for v in parts(m):
+            pass_on(v, step)
 
     def span(part, position):
         if part == 0:
@@ -405,39 +493,50 @@
             ref = new.at[m, 0, span(part, flipped(pos, step))]
         return remote(ref, ref, all_s.at[m, step, part], all_r.at[m, step, part], side)
 
-    def last_step(m):
-        return steps + 1 if m == TWO else steps
+    def last_step(v):
+        return steps + 1 if v // SPLIT == TWO else steps
 
     def renew(m):
-        send_sum(m, steps - 1).wait_recv()
-        grad = total[m, starts[-1]] + landed[m, offset(steps - 1)].astype(jnp.float32)
+        updates, square = [], 0.0
+        for v in parts(m):
+            send_sum(v, steps - 1).wait_recv()
+            grad = total[v, starts[-1]] + landed[v, offset(steps - 1)].astype(jnp.float32)
+            updates.append(old_own[m, :, lanes_of(v)] - grad)
+            square += jnp.sum(updates[-1] * updates[-1], axis=1, keepdims=True)
         old = old_own[m]
-        update = old - grad
         old_len = jnp.sqrt(jnp.sum(old * old, axis=1, keepdims=True))
-        new_len = jnp.sqrt(jnp.sum(update * update, axis=1, keepdims=True) + EPS)
-        new[m, 0, pos] = (update * (old_len / new_len)).astype(jnp.bfloat16)
-        for step in range(last_step(m)):
-            go(send_new(m, step, 0))
-
-    pass_on(TWO, 1)
+        ratio = old_len / jnp.sqrt(square + EPS)
+        for v, update in zip(parts(m), updates):
+            new[v, 0, pos] = (update * ratio).astype(jnp.bfloat16)
+            for step in range(last_step(v)):
+                go(send_new(v, step, 0))
+
+    pass_all(TWO, 1)
+    deltas(b)
     keep_own(ONE)
-    pass_on(ONE, 1)
+    pass_all(ONE, 1)
     keep_own(THREE)
-    pass_on(THREE, 1)
+    pass_all(THREE, 1)
     keep_old(TWO)
     for step in range(2, steps):
         for m in order:
-            pass_on(m, step)
+            pass_all(m, step)
     for m in order:
         renew(m)
 
     dim = width // ATT_HEADS
     scale = 1.0 / math.sqrt(dim)
 
-    @pl.when(me != 0)
-    def _():
-        for copy in halo:
-            copy.wait_recv()
+    each_halo(
+        lambda i: halo_from(i, None).wait_recv(),
+        lambda i: halo_from(i, 0).wait_recv(),
+        lambda i: halo_from(i, 1).wait_recv(),
+        seg_copy.wait_recv,
+        core == 1,
+        (core == 0) & (x == 0) & (me != 0),
+        (core == 0) & (me != 0),
+        me != 0,
+    )
 
     def attend(first_head, last_head):
         row = lax.broadcasted_iota(jnp.int32, (tokens, tokens), 0)
@@ -473,46 +572,52 @@
 
         lax.fori_loop(first_head, last_head, one, 0)
 
+    def query_dot(m, rows_q):
+        return sum(nt_dot(rows_q[:, lanes_of(v)], flat(new[v, 0])) for v in parts(m))
+
     def mixed(place_from):
         slots = pl.ds(place_from * 2, 2)
-        rows_q = qbuf[slots].reshape(2 * tokens, feats)
         b_one = asum[ONE, slots].reshape(2 * tokens, cols)
-        b_three = nt_dot(rows_q, flat(new[THREE, 0]))
+        b_three = query_dot(THREE, qbuf[slots].reshape(2 * tokens, feats))
         return (jax.nn.silu(b_one) * b_three).astype(jnp.bfloat16)
 
-    slots = len(order) * steps - 1
-    for slot, (step, m) in enumerate((step, m) for step in range(steps) for m in order):
+    turns = [(step, m, v) for step in range(steps) for m in order for v in parts(m)]
+    slots = len(turns) - 2
+    for slot, (step, m, v) in enumerate(turns):
         for part in range(step + 1):
-            new_there(m, step, part).wait_recv()
-        for later in range(step + 1, last_step(m)):
-            go(send_new(m, later, step + 1))
+            new_there(v, step, part).wait_recv()
+        for later in range(step + 1, last_step(v)):
+            go(send_new(v, later, step + 1))
         if slot < slots:
             attend(ATT_HEADS * slot // slots, ATT_HEADS * (slot + 1) // slots)
-        if (m, step) == (ONE, steps - 1):
+        if (step, v) == (steps - 1, parts(ONE)[-1]):
             take_tokens(2)
-            asum[ONE] = nt_dot(
-                qbuf[...].reshape(4 * tokens, feats), flat(new[ONE, 0])
-            ).reshape(4, tokens, cols)
+            rows_q = qbuf[...].reshape(4 * tokens, feats)
+            asum[ONE] = query_dot(ONE, rows_q).reshape(4, tokens, cols)
 
     z_send[...] = mixed(1 - a)
     z_copy = remote(z_send, z_peer, end_s.at[0], end_r.at[0], pair)
     go(z_copy)
     z_own[...] = mixed(a)
-    for part in range(steps + 1):
-        new_there(TWO, steps, part).wait_recv()
+    for v in parts(TWO):
+        for part in range(steps + 1):
+            new_there(v, steps, part).wait_recv()
     z_copy.wait_recv()
 
-    def fast_rows(c):
+    def fast_rows(c, v):
         at = pl.ds(pl.multiple_of(c * tokens, tokens), tokens)
-        value = dot(z_own[at, :], flat(new[TWO, 0])) + dot(z_peer[at, :], flat(new[TWO, 1]))
+        value = dot(z_own[at, :], flat(new[v, 0])) + dot(z_peer[at, :], flat(new[v, 1]))
         return value.astype(jnp.bfloat16)
 
-    o_send[...] = fast_rows(other)
+    for v in parts(TWO):
+        o_send[:, lanes_of(v)] = fast_rows(other, v)
     out_copy = remote(
         o_send, out_ref.at[:, own_lanes(core)], end_s.at[1], end_r.at[1], partner
     )
     go(out_copy)
-    out_ref[:, own_lanes(core)] = fast_rows(core)
+    for v in parts(TWO):
+        lanes = pl.ds(pl.multiple_of(core * feats + v % SPLIT * wide, wide), wide)
+        out_ref[:, lanes] = fast_rows(core, v)
     theirs = out_ref.at[:, own_lanes(other)]
     remote(theirs, theirs, end_s.at[1], end_r.at[1], partner).wait_recv()
 
@@ -529,10 +634,16 @@
         def _():
             first(m, 0).wait_send()
 
-    @pl.when(me != count - 1)
-    def _():
-        for copy in halo:
-            copy.wait_send()
+    each_halo(
+        lambda i: halo(i, None).wait_send(),
+        lambda i: halo(i, 0).wait_send(),
+        lambda i: halo(i, 1).wait_send(),
+        seg_copy.wait_send,
+        core == 0,
+        sends_zero,
+        sends_one,
+        me != count - 1,
+    )
 
 
 def per_device(queries, keys, values, segment, rates, fast_one, fast_three, fast_two):
@@ -546,14 +657,20 @@
     cols = hidden // 2
     blocks = 2 * lines
     unit = cols // blocks
+    wide = feats // SPLIT
     bf16, f32 = jnp.bfloat16, jnp.float32
     dma = pltpu.SemaphoreType.DMA
+    operands = (
+        fast_one, fast_three, fast_two, queries, keys, values, segment.reshape(1, tokens), rates.T
+    )
     return pl.pallas_call(
         functools.partial(kernel, count),
         out_shape=[jax.ShapeDtypeStruct(queries.shape, bf16)] * 2,
-        in_specs=[pl.BlockSpec(memory_space=pltpu.VMEM)] * 8,
+        in_specs=[pl.BlockSpec(memory_space=pltpu.HBM)] * 8,
         out_specs=[pl.BlockSpec(memory_space=pltpu.VMEM)] * 2,
-        scratch_shapes=[
+        scratch_shapes=[pltpu.VMEM(one.shape, one.dtype) for one in operands]
+        + [
+            dma((8,)),
             pltpu.VMEM((3, count // 4, 2 * rows, cols), bf16),
             pltpu.VMEM((4, tokens, feats), bf16),
             pltpu.VMEM((4, tokens, feats), bf16),
@@ -562,12 +679,12 @@
             pltpu.VMEM((FAST_HEADS, 8, tokens), f32),
             pltpu.VMEM((3, 4, tokens, cols), f32),
             pltpu.VMEM((3, cols, 4 * tokens), bf16),
-            pltpu.VMEM((3, lines, unit, feats), f32),
-            pltpu.VMEM((3, blocks, unit, feats), bf16),
-            pltpu.VMEM((3, blocks, unit, feats), bf16),
+            pltpu.VMEM((3 * SPLIT, lines, unit, wide), f32),
+            pltpu.VMEM((3 * SPLIT, blocks, unit, wide), bf16),
+            pltpu.VMEM((3 * SPLIT, blocks, unit, wide), bf16),
             pltpu.VMEM((3, unit, feats), f32),
             pltpu.VMEM((lines, unit, feats), f32),
-            pltpu.VMEM((3, 2, blocks, unit, feats), bf16),
+            pltpu.VMEM((3 * SPLIT, 2, blocks, unit, wide), bf16),
             pltpu.VMEM((2 * tokens, cols), bf16),
             pltpu.VMEM((2 * tokens, cols), bf16),
             pltpu.VMEM((2 * tokens, cols), bf16),
@@ -586,21 +703,19 @@
             dma((3, 2, half)),
             dma((4, 3)),
             dma((4, 3)),
-            dma((3, steps)),
-            dma((3, steps)),
-            dma((3, steps + 1, steps + 1)),
-            dma((3, steps + 1, steps + 1)),
+            dma((3 * SPLIT, steps)),
+            dma((3 * SPLIT, steps)),
+            dma((3 * SPLIT, steps + 1, steps + 1)),
+            dma((3 * SPLIT, steps + 1, steps + 1)),
             dma((2,)),
             dma((2,)),
-            dma((3,)),
-            dma((3,)),
+            dma((5,)),
+            dma((5,)),
         ],
         compiler_params=pltpu.CompilerParams(
-            collective_id=0, has_side_effects=True
+            collective_id=0, has_side_effects=True, vmem_limit_bytes=40 << 20
         ),
-    )(
-        fast_one, fast_three, fast_two, queries, keys, values, segment.reshape(1, tokens), rates.T
-    )
+    )(*[pltpu.with_memory_space_constraint(one, pltpu.HBM) for one in operands])
 
 
 def solution(mesh):

time: 90.4 us -> 86.7 us (0.959)
  Pallas kernels: 86.8 us -> 84.3 us
  local copies, waits for them, and re-layouts: 2.74 us -> 1.59 us
    pallas_call x1, Pallas kernels: 86.8 us -> 84.3 us  [per_device(): pl.pallas_call(functools.partial(kernel, count), out_shape=[jax.ShapeDtyp...]
    unnamed x4 -> x2, local copies, waits for them, and re-layouts: 2.74 us -> 1.59 us
where the time goes in v3:
time: 86.7 us; the launch traced here: 86.5 us
  Pallas kernels  84.3 us (97%)
  local copies, waits for them, and re-layouts  1.59 us (2%)
    pallas_call x1, Pallas kernels, per_device(): pl.pallas_call(functools.partial(kernel, count), out_shape=[jax.ShapeDtyp...  84.3 us

profile of v3, /device:TPU:7, one launch (start us, length us, event | category | flops | bytes accessed | tf_op | source)
XLA Modules:
  0.0 86.5 jit_solution(8695191325169062188)
XLA Ops:
  0.6 84.3 %shard_map.95 = (bf16[128,2048]{1,0:T(8,128)(2,1)S(1)}, bf16[128,2048]{1,0:T(8,128)(2,1)S(1)}) custom-call(bf16[64,512]{1,0:T(8,128)(2,1)} %refs_0_.1, bf16[64,512]{1,0:T(8,128)(2,1)} %refs_1_.1, bf16[64,512]{1,0:T(8,128)(2,1)} %refs_2_.1, bf16[128,2048]{1,0:T(8,128)(2,1)} %refs_3_.1, bf16[128,2048]{1,0:T(8,128)(2,1)} %refs_4_.1, bf16[128,2048]{1,0:T(8,128)(2,1)} %refs_5_.1, ...), custom_call_target="tpu_custom_call" | custom-call | tf_op jit(solution)/shard_map/pallas_call | solution.py:666
  84.9 0.8 copy.12
  85.7 0.8 copy.13

commit v4 on v3

--- a/solution.py
+++ b/solution.py
@@ -73,9 +73,9 @@
     q_ref, k_ref, v_ref, seg_ref, rate_ref = loaded[3:8]
     (
         wbuf, kbuf, vbuf, qbuf, rbuf, rsend, asum, hid, total, staged, landed, old_own, old_all, new,
-        z_own, z_peer, z_send, o_send, old_k, old_v, old_seg,
+        z_own, z_peer, z_send, o_send, old_k, old_v, old_seg, relay,
         first_s, first_r, first_l, mirror_s, mirror_r, mate_s, mate_r, side_s, side_r,
-        tok_s, tok_r, sum_s, sum_r, all_s, all_r, end_s, end_r, halo_s, halo_r,
+        tok_s, tok_r, sum_s, sum_r, all_s, all_r, end_s, end_r, halo_s, halo_r, up_s, up_r,
     ) = refs[19:]
 
     lines = count // 8
@@ -128,7 +128,7 @@
     plane = line * 8
     known = [plane + lax.rem(me - plane + i, 8) for i in range(1, 8)]
     known += [mirror] + [mate(i) for i in range(1, half)]
-    known += [around(i) for i in (1, -1, 4, -4, 5, -5)]
+    known += [around(i) for i in (1, -1, 8, -8)]
     for one in known:
         pl.semaphore_signal(
             barrier, inc=1, device_id={"tok": one}, device_id_type=pl.DeviceIdType.MESH
@@ -353,6 +353,54 @@
 
         lax.fori_loop(0, 4, one, 0)
 
+    seg_copy = remote(seg_ref, old_seg, halo_s.at[4], halo_r.at[4], after)
+    kinds = ((k_ref, kbuf, old_k), (v_ref, vbuf, old_v))
+
+    def upward(i):
+        src = kinds[i][1].at[3]
+        return remote(src, relay.at[i], up_s.at[i], up_r.at[i], around(8))
+
+    def halo(i, group, relayed=False):
+        ref, buf, old = kinds[i]
+        if group is None:
+            return remote(ref, old, halo_s.at[i], halo_r.at[i], partner)
+        at = old.at[:, pl.ds(group * feats, feats)]
+        if group == 0:
+            slot, to = 3, device(line, 0, 1 - y, 0)
+        else:
+            slot, to = (y + x - 2 * x * y) * 2 + 1, device(line, 1 - x, y, 0)
+        src = relay.at[i] if relayed else buf.at[slot]
+        return remote(src, at, halo_s.at[i * 2 + group], halo_r.at[i * 2 + group], to)
+
+    def halo_from(i, group):
+        if group is None:
+            return halo(i, None)
+        at = kinds[i][2].at[:, pl.ds(group * feats, feats)]
+        return remote(at, at, halo_s.at[i * 2 + group], halo_r.at[i * 2 + group], partner)
+
+    edge_zero = (core == 0) & (x == 0) & (y == 1)
+    edge_one = (core == 1) & (x == 1) & (y == 0)
+    edge = edge_zero | edge_one
+    plain_zero = (core == 0) & (x == 0) & (y == 0)
+    plain_one = (core == 1) & jnp.logical_not(edge_one)
+
+    def both(predicate, act):
+        @pl.when(predicate)
+        def _():
+            for i in range(2):
+                act(i)
+
+    def halo_sends(act):
+        both(core == 0, lambda i: act(halo(i, None)))
+        both(plain_zero, lambda i: act(halo(i, 0)))
+        both(plain_one, lambda i: act(halo(i, 1)))
+        both(edge_zero & (line > 0), lambda i: act(halo(i, 0, True)))
+        both(edge_one & (line > 0), lambda i: act(halo(i, 1, True)))
+
+        @pl.when(me != count - 1)
+        def _():
+            act(seg_copy)
+
     def project(m):
         weight_there(m)
         rows_in = all_values() if m == TWO else all_keys()
@@ -364,6 +412,7 @@
     project(THREE)
     weigh(1 - b)
     take_tokens(1)
+    both(edge & (line < lines - 1), lambda i: upward(i).start())
     send_away(TWO)
     weigh(b)
     keep_own(TWO)
@@ -375,62 +424,8 @@
     send_away(THREE)
     send_tokens(2)
 
-    seg_copy = remote(seg_ref, old_seg, halo_s.at[4], halo_r.at[4], after)
-    kinds = ((k_ref, kbuf, old_k), (v_ref, vbuf, old_v))
-
-    def halo(i, group):
-        ref, buf, old = kinds[i]
-        if group is None:
-            return remote(ref, old, halo_s.at[i], halo_r.at[i], partner)
-        at = old.at[:, pl.ds(group * feats, feats)]
-        if group == 0:
-            slot, to = 3, device(lax.rem(line + y, lines), 0, 1 - y, 0)
-        else:
-            slot = (y + x - 2 * x * y) * 2 + 1
-            to = device(lax.rem(line + x * (1 - y), lines), 1 - x, y, 0)
-        return remote(buf.at[slot], at, halo_s.at[i * 2 + group], halo_r.at[i * 2 + group], to)
-
-    def halo_from(i, group):
-        ref, buf, old = kinds[i]
-        if group is None:
-            return halo(i, None)
-        at = old.at[:, pl.ds(group * feats, feats)]
-        return remote(at, at, halo_s.at[i * 2 + group], halo_r.at[i * 2 + group], partner)
-
-    last_line = line == lines - 1
-    sends_zero = (core == 0) & (x == 0) & jnp.logical_not((y == 1) & last_line)
-    sends_one = (core == 1) & jnp.logical_not((x == 1) & (y == 0) & last_line)
-
-    def each_halo(act_inner, act_zero, act_one, act_seg, inner, zero, one, seg):
-        @pl.when(inner)
-        def _():
-            for i in range(2):
-                act_inner(i)
-
-        @pl.when(zero)
-        def _():
-            for i in range(2):
-                act_zero(i)
-
-        @pl.when(one)
-        def _():
-            for i in range(2):
-                act_one(i)
-
-        @pl.when(seg)
-        def _():
-            act_seg()
-
-    each_halo(
-        lambda i: halo(i, None).start(),
-        lambda i: halo(i, 0).start(),
-        lambda i: halo(i, 1).start(),
-        seg_copy.start,
-        core == 0,
-        sends_zero,
-        sends_one,
-        me != count - 1,
-    )
+    both(edge & (line > 0), lambda i: upward(i).wait_recv())
+    halo_sends(lambda copy: copy.start())
 
     @pl.when(me == 0)
     def _():
@@ -527,16 +522,13 @@
     dim = width // ATT_HEADS
     scale = 1.0 / math.sqrt(dim)
 
-    each_halo(
-        lambda i: halo_from(i, None).wait_recv(),
-        lambda i: halo_from(i, 0).wait_recv(),
-        lambda i: halo_from(i, 1).wait_recv(),
-        seg_copy.wait_recv,
-        core == 1,
-        (core == 0) & (x == 0) & (me != 0),
-        (core == 0) & (me != 0),
-        me != 0,
-    )
+    both(core == 1, lambda i: halo_from(i, None).wait_recv())
+    both((core == 0) & (x == 0) & (me != 0), lambda i: halo_from(i, 0).wait_recv())
+    both((core == 0) & (me != 0), lambda i: halo_from(i, 1).wait_recv())
+
+    @pl.when(me != 0)
+    def _():
+        seg_copy.wait_recv()
 
     def attend(first_head, last_head):
         row = lax.broadcasted_iota(jnp.int32, (tokens, tokens), 0)
@@ -634,16 +626,8 @@
         def _():
             first(m, 0).wait_send()
 
-    each_halo(
-        lambda i: halo(i, None).wait_send(),
-        lambda i: halo(i, 0).wait_send(),
-        lambda i: halo(i, 1).wait_send(),
-        seg_copy.wait_send,
-        core == 0,
-        sends_zero,
-        sends_one,
-        me != count - 1,
-    )
+    halo_sends(lambda copy: copy.wait_send())
+    both(edge & (line < lines - 1), lambda i: upward(i).wait_send())
 
 
 def per_device(queries, keys, values, segment, rates, fast_one, fast_three, fast_two):
@@ -692,6 +676,7 @@
             pltpu.VMEM(keys.shape, bf16),
             pltpu.VMEM(values.shape, bf16),
             pltpu.VMEM((1, tokens), jnp.int32),
+            pltpu.VMEM((2, tokens, feats), bf16),
             dma((3, 4)),
             dma((3, 4, 2)),
             dma((3,)),
@@ -711,6 +696,8 @@
             dma((2,)),
             dma((5,)),
             dma((5,)),
+            dma((2,)),
+            dma((2,)),
         ],
         compiler_params=pltpu.CompilerParams(
             collective_id=0, has_side_effects=True, vmem_limit_bytes=40 << 20

time: 86.7 us -> 83.9 us (0.968)
  the two profiles are of different devices: /device:TPU:7 before, /device:TPU:1 now
where the time goes in v4:
time: 83.9 us; the launch traced here: 83 us
  Pallas kernels  80.8 us (96%)
  local copies, waits for them, and re-layouts  1.59 us (2%)
    pallas_call x1, Pallas kernels, per_device(): pl.pallas_call(functools.partial(kernel, count), out_shape=[jax.ShapeDtyp...  80.8 us

profile of v4, /device:TPU:1, one launch (start us, length us, event | category | flops | bytes accessed | tf_op | source)
XLA Modules:
  0.0 83.0 jit_solution(8493511005916039641)
XLA Ops:
  0.6 80.8 %shard_map.95 = (bf16[128,2048]{1,0:T(8,128)(2,1)S(1)}, bf16[128,2048]{1,0:T(8,128)(2,1)S(1)}) custom-call(bf16[64,512]{1,0:T(8,128)(2,1)} %refs_0_.1, bf16[64,512]{1,0:T(8,128)(2,1)} %refs_1_.1, bf16[64,512]{1,0:T(8,128)(2,1)} %refs_2_.1, bf16[128,2048]{1,0:T(8,128)(2,1)} %refs_3_.1, bf16[128,2048]{1,0:T(8,128)(2,1)} %refs_4_.1, bf16[128,2048]{1,0:T(8,128)(2,1)} %refs_5_.1, ...), custom_call_target="tpu_custom_call" | custom-call | tf_op jit(solution)/shard_map/pallas_call | solution.py:650
  81.4 0.8 copy.12
  82.2 0.8 copy.13

commit v5 on v4

--- a/solution.py
+++ b/solution.py
@@ -16,6 +16,7 @@
 ONE, THREE, TWO = 0, 1, 2
 WIDE = (TWO,)
 SPLIT = 2
+PAIR = -1
 
 
 def device(line, x, y, core):
@@ -64,6 +65,25 @@
     if unit % 16 == 0:
         return blocks.reshape(n * unit, width)
     return blocks.astype(jnp.float32).reshape(n * unit, width).astype(jnp.bfloat16)
+
+
+def merged(regions):
+    regions = sorted((which, offs // size * size, size) for which, offs, size in regions)
+    for which, offs, size in regions:
+        twin = (which, offs ^ size, size)
+        if twin in regions:
+            rest = [one for one in regions if one not in ((which, offs, size), twin)]
+            return merged(rest + [(which, min(offs, offs ^ size), 2 * size)])
+    return regions
+
+
+def spread_plan(steps, moved):
+    groups, plan = [[(0, 0, 1)]], []
+    for step in steps:
+        known = [(group, region) for group, held in enumerate(groups) for region in held]
+        plan.append([((group, i), region) for i, (group, region) in enumerate(known)])
+        groups.append(merged([moved(region, step) for _, region in known]))
+    return plan
 
 
 def kernel(count, *refs):
@@ -353,6 +373,33 @@
 
         lax.fori_loop(0, 4, one, 0)
 
+    order = (TWO, ONE, THREE)
+
+    def pass_on(m, step):
+        size = lines >> step
+        bit = line_bit[step - 1]
+        kept, away = starts[step], starts[step - 1] + (1 - bit) * size
+        shift = offset(step - 1) - starts[step - 1]
+        send_sum(m, step - 1).wait_recv()
+
+        def stage(i, carry):
+            value = total[m, away + i] + landed[m, shift + away + i].astype(jnp.float32)
+            staged[m, offset(step) + i] = value.astype(jnp.bfloat16)
+            return carry
+
+        def hold(i, carry):
+            value = total[m, kept + i] + landed[m, shift + kept + i].astype(jnp.float32)
+            total[m, kept + i] = value
+            return carry
+
+        lax.fori_loop(0, size, stage, 0)
+        go(send_sum(m, step))
+        lax.fori_loop(0, size, hold, 0)
+
+    def pass_all(m, step):
+        for v in parts(m):
+            pass_on(v, step)
+
     seg_copy = remote(seg_ref, old_seg, halo_s.at[4], halo_r.at[4], after)
     kinds = ((k_ref, kbuf, old_k), (v_ref, vbuf, old_v))
 
@@ -421,6 +468,7 @@
     project(TWO)
     deltas(1 - b)
     send_away(ONE)
+    pass_all(TWO, 1)
     send_away(THREE)
     send_tokens(2)
 
@@ -438,58 +486,53 @@
         for _, buf, old in kinds:
             old[:, 0:feats] = buf[1]
 
-    order = (TWO, ONE, THREE)
-
-    def pass_on(m, step):
-        size = lines >> step
-        bit = line_bit[step - 1]
-        kept, away = starts[step], starts[step - 1] + (1 - bit) * size
-        shift = offset(step - 1) - starts[step - 1]
-        send_sum(m, step - 1).wait_recv()
-
-        def stage(i, carry):
-            value = total[m, away + i] + landed[m, shift + away + i].astype(jnp.float32)
-            staged[m, offset(step) + i] = value.astype(jnp.bfloat16)
-            return carry
-
-        def hold(i, carry):
-            value = total[m, kept + i] + landed[m, shift + kept + i].astype(jnp.float32)
-            total[m, kept + i] = value
-            return carry
-
-        lax.fori_loop(0, size, stage, 0)
-        go(send_sum(m, step))
-        lax.fori_loop(0, size, hold, 0)
-
-    def pass_all(m, step):
-        for v in parts(m):
-            pass_on(v, step)
-
-    def span(part, position):
-        if part == 0:
-            return pl.ds(position, 1)
-        size = 1 << (part - 1)
-        return pl.ds(flipped(lax.div(position, jnp.int32(size)), 0) * size, size)
-
-    def send_new(m, step, part):
-        src = new.at[m, 0, span(part, pos)]
-        if step == steps:
-            dst, to = new.at[m, 1, span(part, pos)], pair
-        elif step == steps - 1:
-            dst, to = src, side
-        else:
-            dst, to = src, in_role(flipped(line, line_bits - 1 - step), a, b, core)
-        return remote(src, dst, all_s.at[m, step, part], all_r.at[m, step, part], to)
-
-    def new_there(m, step, part):
-        if step == steps:
-            ref = new.at[m, 1, span(part, pos)]
-        else:
-            ref = new.at[m, 0, span(part, flipped(pos, step))]
-        return remote(ref, ref, all_s.at[m, step, part], all_r.at[m, step, part], side)
-
-    def last_step(v):
-        return steps + 1 if v // SPLIT == TWO else steps
+    pos_bits = line_bit[::-1] + [b]
+    low = list(range(line_bits - 1))
+    orders = {
+        ONE: low + [line_bits - 1, line_bits],
+        THREE: low + [line_bits - 1, line_bits],
+        TWO: low + [PAIR, line_bits - 1, line_bits],
+    }
+
+    def moved(region, step):
+        which, offs, size = region
+        return (1 - which, offs, size) if step == PAIR else (which, offs ^ (1 << step), size)
+
+    plans = {m: spread_plan(orders[m], moved) for m in order}
+
+    def block_of(v, region):
+        which, offs, size = region
+        start = jnp.int32(0)
+        for i, bit in enumerate(pos_bits):
+            if (1 << i) >= size:
+                start += (1 - bit if (offs >> i) & 1 else bit) * (1 << i)
+        return new.at[v, which, pl.ds(start, size)]
+
+    def partner_at(step):
+        if step == PAIR:
+            return pair
+        if step == line_bits:
+            return side
+        return in_role(flipped(line, line_bits - 1 - step), a, b, core)
+
+    def new_copy(v, turn, index, src, dst):
+        to = partner_at(orders[v // SPLIT][turn])
+        return remote(src, dst, all_s.at[v, turn, index], all_r.at[v, turn, index], to)
+
+    def send_group(v, group):
+        m = v // SPLIT
+        for turn in range(group, len(orders[m])):
+            for index, region in plans[m][turn]:
+                if index[0] != group:
+                    continue
+                dst = region if orders[m][turn] != PAIR else (1 - region[0],) + region[1:]
+                go(new_copy(v, turn, index[1], block_of(v, region), block_of(v, dst)))
+
+    def new_wait(v, turn):
+        m = v // SPLIT
+        for index, region in plans[m][turn]:
+            ref = block_of(v, moved(region, orders[m][turn]))
+            new_copy(v, turn, index[1], ref, ref).wait_recv()
 
     def renew(m):
         updates, square = [], 0.0
@@ -503,10 +546,8 @@
         ratio = old_len / jnp.sqrt(square + EPS)
         for v, update in zip(parts(m), updates):
             new[v, 0, pos] = (update * ratio).astype(jnp.bfloat16)
-            for step in range(last_step(v)):
-                go(send_new(v, step, 0))
-
-    pass_all(TWO, 1)
+            send_group(v, 0)
+
     deltas(b)
     keep_own(ONE)
     pass_all(ONE, 1)
@@ -573,16 +614,20 @@
         b_three = query_dot(THREE, qbuf[slots].reshape(2 * tokens, feats))
         return (jax.nn.silu(b_one) * b_three).astype(jnp.bfloat16)
 
-    turns = [(step, m, v) for step in range(steps) for m in order for v in parts(m)]
+    turns = [
+        (turn, v)
+        for turn in range(steps + 1)
+        for m in order
+        for v in parts(m)
+        if turn < len(orders[m]) and turn < steps
+    ]
     slots = len(turns) - 2
-    for slot, (step, m, v) in enumerate(turns):
-        for part in range(step + 1):
-            new_there(v, step, part).wait_recv()
-        for later in range(step + 1, last_step(v)):
-            go(send_new(v, later, step + 1))
+    for slot, (turn, v) in enumerate(turns):
+        new_wait(v, turn)
+        send_group(v, turn + 1)
         if slot < slots:
             attend(ATT_HEADS * slot // slots, ATT_HEADS * (slot + 1) // slots)
-        if (step, v) == (steps - 1, parts(ONE)[-1]):
+        if (turn, v) == (steps - 1, parts(ONE)[-1]):
             take_tokens(2)
             rows_q = qbuf[...].reshape(4 * tokens, feats)
             asum[ONE] = query_dot(ONE, rows_q).reshape(4, tokens, cols)
@@ -592,8 +637,7 @@
     go(z_copy)
     z_own[...] = mixed(a)
     for v in parts(TWO):
-        for part in range(steps + 1):
-            new_there(v, steps, part).wait_recv()
+        new_wait(v, steps)
     z_copy.wait_recv()
 
     def fast_rows(c, v):
@@ -690,8 +734,8 @@
             dma((4, 3)),
             dma((3 * SPLIT, steps)),
             dma((3 * SPLIT, steps)),
-            dma((3 * SPLIT, steps + 1, steps + 1)),
-            dma((3 * SPLIT, steps + 1, steps + 1)),
+            dma((3 * SPLIT, steps + 1, 2 * steps)),
+            dma((3 * SPLIT, steps + 1, 2 * steps)),
             dma((2,)),
             dma((2,)),
             dma((5,)),

time: 83.9 us -> 81 us (0.965)
  Pallas kernels: 80.8 us -> 78.6 us
    pallas_call x1, Pallas kernels: 80.8 us -> 78.6 us  [per_device(): pl.pallas_call(functools.partial(kernel, count), out_shape=[jax.ShapeDtyp...]
where the time goes in v5:
time: 81 us; the launch traced here: 80.8 us
  Pallas kernels  78.6 us (97%)
  local copies, waits for them, and re-layouts  1.59 us (2%)
    pallas_call x1, Pallas kernels, per_device(): pl.pallas_call(functools.partial(kernel, count), out_shape=[jax.ShapeDtyp...  78.6 us

profile of v5, /device:TPU:1, one launch (start us, length us, event | category | flops | bytes accessed | tf_op | source)
XLA Modules:
  0.0 80.8 jit_solution(11923193961988469632)
XLA Ops:
  0.6 78.6 %shard_map.95 = (bf16[128,2048]{1,0:T(8,128)(2,1)S(1)}, bf16[128,2048]{1,0:T(8,128)(2,1)S(1)}) custom-call(bf16[64,512]{1,0:T(8,128)(2,1)} %refs_0_.1, bf16[64,512]{1,0:T(8,128)(2,1)} %refs_1_.1, bf16[64,512]{1,0:T(8,128)(2,1)} %refs_2_.1, bf16[128,2048]{1,0:T(8,128)(2,1)} %refs_3_.1, bf16[128,2048]{1,0:T(8,128)(2,1)} %refs_4_.1, bf16[128,2048]{1,0:T(8,128)(2,1)} %refs_5_.1, ...), custom_call_target="tpu_custom_call" | custom-call | tf_op jit(solution)/shard_map/pallas_call | solution.py:694
  79.2 0.8 copy.12
  80.0 0.8 copy.13

commit v6 on v5

--- a/solution.py
+++ b/solution.py
@@ -645,17 +645,19 @@
         value = dot(z_own[at, :], flat(new[v, 0])) + dot(z_peer[at, :], flat(new[v, 1]))
         return value.astype(jnp.bfloat16)
 
+    def out_copy(v, group):
+        lanes = pl.ds(pl.multiple_of(group * feats + v % SPLIT * wide, wide), wide)
+        src, at = o_send.at[:, pl.ds(v % SPLIT * wide, wide)], 1 + v % SPLIT
+        return remote(src, out_ref.at[:, lanes], end_s.at[at], end_r.at[at], partner)
+
     for v in parts(TWO):
         o_send[:, lanes_of(v)] = fast_rows(other, v)
-    out_copy = remote(
-        o_send, out_ref.at[:, own_lanes(core)], end_s.at[1], end_r.at[1], partner
-    )
-    go(out_copy)
+        go(out_copy(v, core))
     for v in parts(TWO):
         lanes = pl.ds(pl.multiple_of(core * feats + v % SPLIT * wide, wide), wide)
         out_ref[:, lanes] = fast_rows(core, v)
-    theirs = out_ref.at[:, own_lanes(other)]
-    remote(theirs, theirs, end_s.at[1], end_r.at[1], partner).wait_recv()
+    for v in parts(TWO):
+        out_copy(v, other).wait_recv()
 
     for copy in started:
         copy.wait_send()
@@ -736,8 +738,8 @@
             dma((3 * SPLIT, steps)),
             dma((3 * SPLIT, steps + 1, 2 * steps)),
             dma((3 * SPLIT, steps + 1, 2 * steps)),
-            dma((2,)),
-            dma((2,)),
+            dma((1 + SPLIT,)),
+            dma((1 + SPLIT,)),
             dma((5,)),
             dma((5,)),
             dma((2,)),

time: 81 us -> 81 us (level)
  no operation moved by 1% of the time
where the time goes in v6:
time: 81 us; the launch traced here: 80.8 us
  Pallas kernels  78.6 us (97%)
  local copies, waits for them, and re-layouts  1.59 us (2%)
    pallas_call x1, Pallas kernels, per_device(): pl.pallas_call(functools.partial(kernel, count), out_shape=[jax.ShapeDtyp...  78.6 us

profile of v6, /device:TPU:1, one launch (start us, length us, event | category | flops | bytes accessed | tf_op | source)
XLA Modules:
  0.0 80.8 jit_solution(17240922626461025376)
XLA Ops:
  0.6 78.6 %shard_map.95 = (bf16[128,2048]{1,0:T(8,128)(2,1)S(1)}, bf16[128,2048]{1,0:T(8,128)(2,1)S(1)}) custom-call(bf16[64,512]{1,0:T(8,128)(2,1)} %refs_0_.1, bf16[64,512]{1,0:T(8,128)(2,1)} %refs_1_.1, bf16[64,512]{1,0:T(8,128)(2,1)} %refs_2_.1, bf16[128,2048]{1,0:T(8,128)(2,1)} %refs_3_.1, bf16[128,2048]{1,0:T(8,128)(2,1)} %refs_4_.1, bf16[128,2048]{1,0:T(8,128)(2,1)} %refs_5_.1, ...), custom_call_target="tpu_custom_call" | custom-call | tf_op jit(solution)/shard_map/pallas_call | solution.py:696
  79.2 0.8 copy.12
  80.0 0.8 copy.13
